TPU v7x, 32 devices: a whole 2x2x4 slice. The times are simulated.
32 devices in a mesh: dp: 8 (over z, x), tensor: 4 (over y, core).
Axes of the slice: x: 2, y: 2, z: 4, core: 2. Of those that a mesh axis runs over, the one named last changes fastest.
Arguments:
- tokens: bfloat16 [8192, 1024], P('dp'), may hold values from -6 to 6
- memory: bfloat16 [8192, 1024], P('dp'), may hold values from -6 to 6
- decoder_length: int32 [8], P('dp'), may hold values from 512 to 1024, as said below
- memory_length: int32 [8], P('dp'), may hold values from 512 to 1024, as said below
- self_query: bfloat16 [1024, 1024], P(None, 'tensor'), may hold values from -0.1875 to 0.1875
- self_key: bfloat16 [1024, 1024], P(None, 'tensor'), may hold values from -0.1875 to 0.1875
- self_value: bfloat16 [1024, 1024], P(None, 'tensor'), may hold values from -0.1875 to 0.1875
- self_output: bfloat16 [1024, 1024], P('tensor'), may hold values from -2 to 2
- self_gain: float32 [1024], replicated, may hold values from 0.5 to 1.5
- self_bias: float32 [1024], replicated, may hold values from -3 to 3
- cross_query: bfloat16 [1024, 1024], P(None, 'tensor'), may hold values from -0.1875 to 0.1875
- cross_key: bfloat16 [1024, 1024], P(None, 'tensor'), may hold values from -0.1875 to 0.1875
- cross_value: bfloat16 [1024, 1024], P(None, 'tensor'), may hold values from -0.1875 to 0.1875
- cross_output: bfloat16 [1024, 1024], P('tensor'), may hold values from -2 to 2
- cross_gain: float32 [1024], replicated, may hold values from 0.5 to 1.5
- cross_bias: float32 [1024], replicated, may hold values from -3 to 3
- feed_in: bfloat16 [1024, 4096], P(None, 'tensor'), may hold values from -0.1875 to 0.1875
- feed_out: bfloat16 [4096, 1024], P('tensor'), may hold values from -0.09375 to 0.09375
- feed_gain: float32 [1024], replicated, may hold values from 0.5 to 1.5
- feed_bias: float32 [1024], replicated, may hold values from -3 to 3
- cotangent: bfloat16 [8192, 1024], P('dp'), may hold values from -6 to 6
Outputs:
- output: bfloat16 [8192, 1024], P('dp')
- tokens_grad: float32 [8192, 1024], P('dp')
- memory_grad: float32 [8192, 1024], P('dp')
- self_query_grad: float32 [1024, 1024], P(None, 'tensor')
- self_key_grad: float32 [1024, 1024], P(None, 'tensor')
- self_value_grad: float32 [1024, 1024], P(None, 'tensor')
- self_output_grad: float32 [1024, 1024], P('tensor')
- self_gain_grad: float32 [1024], replicated
- self_bias_grad: float32 [1024], replicated
- cross_query_grad: float32 [1024, 1024], P(None, 'tensor')
- cross_key_grad: float32 [1024, 1024], P(None, 'tensor')
- cross_value_grad: float32 [1024, 1024], P(None, 'tensor')
- cross_output_grad: float32 [1024, 1024], P('tensor')
- cross_gain_grad: float32 [1024], replicated
- cross_bias_grad: float32 [1024], replicated
- feed_in_grad: float32 [1024, 4096], P(None, 'tensor')
- feed_out_grad: float32 [4096, 1024], P('tensor')
- feed_gain_grad: float32 [1024], replicated
- feed_bias_grad: float32 [1024], replicated
Inputs may be any that keep to these rules, and one draw needn't show every extreme that they name: Each item's decoder rows in use are its first decoder_length rows; some item uses all 1024. Each item's memory rows in use are its first memory_length rows; some item uses all 1024.
All inputs are finite; a program needn't handle non-finite values.
Results may differ from a plain program's by a relative error of at most 0.04.
Values may be sent and summed in bfloat16 or wider, within the bound.
A program may use at most 192 MiB of HBM per device.

v0:
```python
import jax
import jax.numpy as jnp
from jax import lax
from jax.sharding import PartitionSpec as P

HD = 64


EPSILON = 1e-05
NEGATIVE = -1e30


def layer_norm(summed, gain, bias):
    center = summed - jnp.mean(summed, axis=-1, keepdims=True)
    spread = jnp.mean(center * center, axis=-1, keepdims=True)
    return center * lax.rsqrt(spread + EPSILON) * gain + bias


def gelu_exact(values):
    return jax.nn.gelu(values, approximate=False)


def product(left, right):
    return jnp.dot(left, right, preferred_element_type=jnp.float32)


def transposed_left(left, right):
    return jnp.einsum("rk,rn->kn", left, right, preferred_element_type=jnp.float32)


def transposed_right(left, right):
    return jnp.einsum("rk,nk->rn", left, right, preferred_element_type=jnp.float32)


def attend_forward(queries, keys, values, allowed):
    rows = queries.shape[0]
    heads = queries.shape[1] // HD
    span = min(512, rows)
    scale = HD ** (-0.5)
    key_heads = keys.reshape(keys.shape[0], heads, HD)
    value_heads = values.reshape(values.shape[0], heads, HD)
    query_blocks = queries.reshape(rows // span, span, heads, HD)
    offsets = jnp.arange(rows // span, dtype=jnp.int32) * span

    def one_block(inputs):
        query_block, offset = inputs
        scores = (
            jnp.einsum("qhd,khd->hqk", query_block, key_heads, preferred_element_type=jnp.float32)
            * scale
        )
        scores = jnp.where(
            allowed(offset + jnp.arange(span, dtype=jnp.int32))[None], scores, NEGATIVE
        )
        highest = jnp.max(scores, axis=-1, keepdims=True)
        raised = jnp.exp(scores - highest)
        total = jnp.sum(raised, axis=-1, keepdims=True)
        shares = (raised / total).astype(jnp.bfloat16)
        mixed = jnp.einsum("hqk,khd->qhd", shares, value_heads, preferred_element_type=jnp.float32)
        return (
            mixed.reshape(span, heads * HD).astype(jnp.bfloat16),
            highest[..., 0] + jnp.log(total[..., 0]),
        )

    mixed, logsum = lax.map(one_block, (query_blocks, offsets))
    return (mixed.reshape(rows, heads * HD), logsum)


def attend_backward(queries, keys, values, logsum, grad_mixed, allowed):
    rows = queries.shape[0]
    heads = queries.shape[1] // HD
    span = min(512, rows)
    scale = HD ** (-0.5)
    key_heads = keys.reshape(keys.shape[0], heads, HD)
    value_heads = values.reshape(values.shape[0], heads, HD)
    query_blocks = queries.reshape(rows // span, span, heads, HD)
    grad_blocks = grad_mixed.reshape(rows // span, span, heads, HD)
    offsets = jnp.arange(rows // span, dtype=jnp.int32) * span

    def one_block(carry, inputs):
        key_total, value_total = carry
        query_block, grad_block, logsum_block, offset = inputs
        scores = (
            jnp.einsum("qhd,khd->hqk", query_block, key_heads, preferred_element_type=jnp.float32)
            * scale
        )
        scores = jnp.where(
            allowed(offset + jnp.arange(span, dtype=jnp.int32))[None], scores, NEGATIVE
        )
        shares = jnp.exp(scores - logsum_block[..., None])
        value_total = value_total + jnp.einsum(
            "hqk,qhd->khd",
            shares.astype(jnp.bfloat16),
            grad_block,
            preferred_element_type=jnp.float32,
        )
        share_grad = jnp.einsum(
            "qhd,khd->hqk", grad_block, value_heads, preferred_element_type=jnp.float32
        )
        score_grad = shares * (share_grad - jnp.sum(shares * share_grad, axis=-1, keepdims=True))
        rounded = score_grad.astype(jnp.bfloat16)
        grad_query = (
            jnp.einsum("hqk,khd->qhd", rounded, key_heads, preferred_element_type=jnp.float32)
            * scale
        )
        key_total = (
            key_total
            + jnp.einsum("hqk,qhd->khd", rounded, query_block, preferred_element_type=jnp.float32)
            * scale
        )
        return ((key_total, value_total), grad_query.reshape(span, heads * HD).astype(jnp.bfloat16))

    zeros = jnp.zeros(key_heads.shape, jnp.float32)
    (key_total, value_total), grad_queries = lax.scan(
        one_block, (zeros, zeros), (query_blocks, grad_blocks, logsum, offsets)
    )
    width = heads * HD
    return (
        grad_queries.reshape(rows, width),
        key_total.reshape(-1, width).astype(jnp.bfloat16),
        value_total.reshape(-1, width).astype(jnp.bfloat16),
    )


def shards(
    tokens,
    memory,
    decoder_length,
    memory_length,
    self_query,
    self_key,
    self_value,
    self_output,
    self_gain,
    self_bias,
    cross_query,
    cross_key,
    cross_value,
    cross_output,
    cross_gain,
    cross_bias,
    feed_in,
    feed_out,
    feed_gain,
    feed_bias,
    cotangent,
):
    rows = tokens.shape[0]
    slots = memory.shape[0]
    row_ids = jnp.arange(rows, dtype=jnp.int32)
    memory_ids = jnp.arange(slots, dtype=jnp.int32)
    decoded = decoder_length[0]
    encoded = memory_length[0]

    def self_allowed(query_ids):
        return (row_ids[None, :] <= query_ids[:, None]) & (row_ids[None, :] < decoded)

    def cross_allowed(query_ids):
        return jnp.broadcast_to((memory_ids < encoded)[None, :], (query_ids.shape[0], slots))

    queries = product(tokens, self_query).astype(jnp.bfloat16)
    keys_self = product(tokens, self_key).astype(jnp.bfloat16)
    values_self = product(tokens, self_value).astype(jnp.bfloat16)
    self_mixed, self_logsum = attend_forward(queries, keys_self, values_self, self_allowed)
    self_added = lax.psum(product(self_mixed, self_output).astype(jnp.bfloat16), "tensor").astype(
        jnp.float32
    )
    first, first_back = jax.vjp(
        layer_norm, tokens.astype(jnp.float32) + self_added, self_gain, self_bias
    )
    first_low = first.astype(jnp.bfloat16)
    cross_queries = product(first_low, cross_query).astype(jnp.bfloat16)
    cross_keys = product(memory, cross_key).astype(jnp.bfloat16)
    cross_values = product(memory, cross_value).astype(jnp.bfloat16)
    cross_mixed, cross_logsum = attend_forward(
        cross_queries, cross_keys, cross_values, cross_allowed
    )
    cross_added = lax.psum(
        product(cross_mixed, cross_output).astype(jnp.bfloat16), "tensor"
    ).astype(jnp.float32)
    second, second_back = jax.vjp(layer_norm, first + cross_added, cross_gain, cross_bias)
    second_low = second.astype(jnp.bfloat16)
    hidden_pre = product(second_low, feed_in)
    hidden_full, gelu_back = jax.vjp(gelu_exact, hidden_pre)
    hidden = hidden_full.astype(jnp.bfloat16)
    feed_added = lax.psum(product(hidden, feed_out).astype(jnp.bfloat16), "tensor").astype(
        jnp.float32
    )
    final, final_back = jax.vjp(layer_norm, second + feed_added, feed_gain, feed_bias)
    output = final.astype(jnp.bfloat16)
    row_mask = (row_ids < decoded).astype(jnp.float32)[:, None]
    grad_third, grad_feed_gain, grad_feed_bias = final_back(
        cotangent.astype(jnp.float32) * row_mask
    )
    feed_low = grad_third.astype(jnp.bfloat16)
    grad_feed_out = transposed_left(hidden, feed_low)
    grad_hidden = transposed_right(feed_low, feed_out)
    grad_pre = gelu_back(grad_hidden)[0].astype(jnp.bfloat16)
    grad_feed_in = transposed_left(second_low, grad_pre)
    grad_second = grad_third + lax.psum(
        transposed_right(grad_pre, feed_in).astype(jnp.bfloat16), "tensor"
    ).astype(jnp.float32)
    grad_second_sum, grad_cross_gain, grad_cross_bias = second_back(grad_second)
    cross_low = grad_second_sum.astype(jnp.bfloat16)
    grad_cross_output = transposed_left(cross_mixed, cross_low)
    grad_cross_mixed = transposed_right(cross_low, cross_output).astype(jnp.bfloat16)
    grad_cross_queries, grad_cross_keys, grad_cross_values = attend_backward(
        cross_queries, cross_keys, cross_values, cross_logsum, grad_cross_mixed, cross_allowed
    )
    grad_cross_query = transposed_left(first_low, grad_cross_queries)
    grad_cross_key = transposed_left(memory, grad_cross_keys)
    grad_cross_value = transposed_left(memory, grad_cross_values)
    first_term = transposed_right(grad_cross_queries, cross_query)
    memory_term = transposed_right(grad_cross_keys, cross_key) + transposed_right(
        grad_cross_values, cross_value
    )
    first_total, memory_grad = (
        lax.psum(first_term.astype(jnp.bfloat16), "tensor").astype(jnp.float32),
        lax.psum(memory_term.astype(jnp.bfloat16), "tensor").astype(jnp.float32),
    )
    grad_first = grad_second_sum + first_total
    grad_first_sum, grad_self_gain, grad_self_bias = first_back(grad_first)
    self_low = grad_first_sum.astype(jnp.bfloat16)
    grad_self_output = transposed_left(self_mixed, self_low)
    grad_self_mixed = transposed_right(self_low, self_output).astype(jnp.bfloat16)
    grad_queries, grad_keys, grad_values = attend_backward(
        queries, keys_self, values_self, self_logsum, grad_self_mixed, self_allowed
    )
    grad_self_query = transposed_left(tokens, grad_queries)
    grad_self_key = transposed_left(tokens, grad_keys)
    grad_self_value = transposed_left(tokens, grad_values)
    input_term = (
        transposed_right(grad_queries, self_query)
        + transposed_right(grad_keys, self_key)
        + transposed_right(grad_values, self_value)
    )
    tokens_grad = grad_first_sum + lax.psum(input_term.astype(jnp.bfloat16), "tensor").astype(
        jnp.float32
    )
    totals = (
        lax.psum(grad_self_query.astype(jnp.bfloat16), "dp").astype(jnp.float32),
        lax.psum(grad_self_key.astype(jnp.bfloat16), "dp").astype(jnp.float32),
        lax.psum(grad_self_value.astype(jnp.bfloat16), "dp").astype(jnp.float32),
        lax.psum(grad_self_output.astype(jnp.bfloat16), "dp").astype(jnp.float32),
        lax.psum(grad_self_gain.astype(jnp.bfloat16), "dp").astype(jnp.float32),
        lax.psum(grad_self_bias.astype(jnp.bfloat16), "dp").astype(jnp.float32),
        lax.psum(grad_cross_query.astype(jnp.bfloat16), "dp").astype(jnp.float32),
        lax.psum(grad_cross_key.astype(jnp.bfloat16), "dp").astype(jnp.float32),
        lax.psum(grad_cross_value.astype(jnp.bfloat16), "dp").astype(jnp.float32),
        lax.psum(grad_cross_output.astype(jnp.bfloat16), "dp").astype(jnp.float32),
        lax.psum(grad_cross_gain.astype(jnp.bfloat16), "dp").astype(jnp.float32),
        lax.psum(grad_cross_bias.astype(jnp.bfloat16), "dp").astype(jnp.float32),
        lax.psum(grad_feed_in.astype(jnp.bfloat16), "dp").astype(jnp.float32),
        lax.psum(grad_feed_out.astype(jnp.bfloat16), "dp").astype(jnp.float32),
        lax.psum(grad_feed_gain.astype(jnp.bfloat16), "dp").astype(jnp.float32),
        lax.psum(grad_feed_bias.astype(jnp.bfloat16), "dp").astype(jnp.float32),
    )
    return (
        output,
        tokens_grad,
        memory_grad,
        totals[0],
        totals[1],
        totals[2],
        totals[3],
        totals[4],
        totals[5],
        totals[6],
        totals[7],
        totals[8],
        totals[9],
        totals[10],
        totals[11],
        totals[12],
        totals[13],
        totals[14],
        totals[15],
    )


def solution(mesh):
    return jax.shard_map(
        shards,
        mesh=mesh,
        in_specs=(
            P("dp", None),
            P("dp", None),
            P("dp"),
            P("dp"),
            P(None, "tensor"),
            P(None, "tensor"),
            P(None, "tensor"),
            P("tensor", None),
            P(),
            P(),
            P(None, "tensor"),
            P(None, "tensor"),
            P(None, "tensor"),
            P("tensor", None),
            P(),
            P(),
            P(None, "tensor"),
            P("tensor", None),
            P(),
            P(),
            P("dp", None),
        ),
        out_specs=(
            P("dp", None),
            P("dp", None),
            P("dp", None),
            P(None, "tensor"),
            P(None, "tensor"),
            P(None, "tensor"),
            P("tensor", None),
            P(),
            P(),
            P(None, "tensor"),
            P(None, "tensor"),
            P(None, "tensor"),
            P("tensor", None),
            P(),
            P(),
            P(None, "tensor"),
            P("tensor", None),
            P(),
            P(),
        ),
        check_vma=False,
    )
```

profile of v0, /device:TPU:0, one launch (start us, length us, event | category | flops | bytes accessed | tf_op | source)
XLA Modules:
  0.0 883.0 jit_solution(9839235483168312248)
XLA Ops:
  7.3 2.5 convolution_convert_fusion.22
  11.2 2.3 copy.52
  13.5 2.3 convolution_convert_fusion.21
  15.8 3.2 convolution_convert_fusion.20
  19.9 22.3 %while.59 = (s32[]{:T(128)}, bf16[2,512,256]{2,1,0:T(8,128)(2,1)}, f32[2,4,512]{2,1,0:T(4,128)S(1)}, s32[2]{0:T(128)S(1)}, s32[]{:T(128)}, /*index=5*/bf16[2,512...) while((s32[]{:T(128)}, bf16[2,512,256]{2,1,0:T(8,128)(2,1)}, ...), condition=%wide.region_3.4_spmd.clone.clone, body=%wide.region_0.3_spmd.clone.clone.sunk | while | flops 563215872 | bytes 32053408 | solution.py:64
  22.2 2.6 fusion.236
  24.8 2.3 fusion.237
  27.2 2.9 fusion.238
  33.3 2.6 fusion.236
  36.0 2.3 fusion.237
  38.3 2.9 fusion.238
  42.1 3.4 convolution_convert_fusion.6
  45.9 2.4 convolution_convert_fusion.18
  48.3 3.2 convolution_convert_fusion.17
  51.6 48.3 %all-reduce.11.cloned.1.call-done = bf16[1024,1024]{1,0:T(8,128)(2,1)} async-done(((bf16[1024,1024]{1,0:T(8,128)(2,1)}), bf16[1024,1024]{1,0:T(8,128)(2,1)}) %all-reduce.11.cloned.1.call-update) | async-done | bytes 2097168 | tf_op jit(solution)/shard_map/psum | solution.py:164
  99.9 3.0 fusion.97
  111.9 18.1 %while.58 = (s32[]{:T(128)}, bf16[2,512,256]{2,1,0:T(8,128)(2,1)}, f32[2,4,512]{2,1,0:T(4,128)S(1)}, s32[]{:T(128)}, bf16[2,512,4,64]{1,3,2,0:T(8,128)(2,1)S(1)}...) while((s32[]{:T(128)}, bf16[2,512,256]{2,1,0:T(8,128)(2,1)}, ...), condition=%wide.region_10.11_spmd.clone, body=%wide.region_7.10_spmd.clone.sunk | while | flops 562166784 | bytes 29954184 | solution.py:64
  116.0 3.1 fusion.232
  125.0 3.1 fusion.232
  130.0 3.2 convolution_convert_fusion.5
  133.8 51.1 %all-reduce.13.cloned.1.call-done = bf16[1024,1024]{1,0:T(8,128)(2,1)} async-done(((bf16[1024,1024]{1,0:T(8,128)(2,1)}), bf16[1024,1024]{1,0:T(8,128)(2,1)}) %all-reduce.13.cloned.1.call-update) | async-done | bytes 2097168 | tf_op jit(solution)/shard_map/psum | solution.py:177
  184.9 3.8 fusion.120
  189.5 13.0 %multiply_convert_fusion.2 = (bf16[1024,1024]{1,0:T(8,128)(2,1)S(1)}, f32[1024,1024]{1,0:T(8,128)}, f32[1024,1024]{1,0:T(8,128)}) fusion(bf16[1024,1024]{1,0:T(8,128)(2,1)S(1)} %copy-done, f32[1024,1024]{1,0:T(8,128)S(1)} %get-tuple-element.626, f32[1024]{0:T(1024)S(1)} %copy-done.77, f32[1024]{0:T(1024)S(1)} %copy-done.69, f32[1024]{0:T(1024)S(1)} %fusion.107, ...), kind=kOutput, calls=%fused_computation.129 | convolution fusion | flops 2220883968 | bytes 16793600 | tf_op jit(solution)/shard_map/dot_general | solution.py:24
  203.8 3.7 convolution_convert_fusion.4
  208.2 50.9 %all-reduce.15.cloned.1.call-done = bf16[1024,1024]{1,0:T(8,128)(2,1)} async-done(((bf16[1024,1024]{1,0:T(8,128)(2,1)}), bf16[1024,1024]{1,0:T(8,128)(2,1)}) %all-reduce.15.cloned.1.call-update) | async-done | bytes 2097168 | tf_op jit(solution)/shard_map/psum | solution.py:185
  259.1 3.7 fusion.118
  264.4 2.8 multiply_reduce_fusion.2
  267.2 3.4 fusion.117
  272.7 3.9 add_convert_fusion.2
  278.0 3.8 convolution_convert_fusion.3
  281.8 6.8 convolution_convert_fusion
  288.6 4.0 convolution_convert_fusion.1
  292.6 40.7 %all-reduce.17.cloned.1.call-done = bf16[1024,1024]{1,0:T(8,128)(2,1)} async-done(((bf16[1024,1024]{1,0:T(8,128)(2,1)}), bf16[1024,1024]{1,0:T(8,128)(2,1)}) %all-reduce.17.cloned.1.call-update) | async-done | bytes 2097168 | tf_op jit(solution)/shard_map/psum | solution.py:199
  333.4 6.0 multiply_reduce_fusion.3
  349.9 30.4 %while.60 = (s32[]{:T(128)}, f32[1024,4,64]{0,2,1:T(8,128)S(1)}, f32[1024,4,64]{0,2,1:T(8,128)}, bf16[2,512,256]{2,1,0:T(8,128)(2,1)}, bf16[2,512,4,64]{1,3,2,0:...) while((s32[]{:T(128)}, f32[1024,4,64]{0,2,1:T(8,128)S(1)}, ...), condition=%wide.region_24.25_spmd.clone, body=%wide.region_22.24_spmd.clone.sunk | while | flops 1375206400 | bytes 71102616 | solution.py:113
  351.9 3.9 fusion.250
  355.7 3.7 multiply_reduce_fusion.13
  366.9 4.2 fusion.250
  371.1 3.7 multiply_reduce_fusion.13
  381.9 3.5 convolution_convert_fusion.2
  385.7 2.7 convolution_convert_fusion.10
  391.5 45.5 %all-reduce.19.cloned.1.call-done = bf16[1024,1024]{1,0:T(8,128)(2,1)} async-done(((bf16[1024,1024]{1,0:T(8,128)(2,1)}), bf16[1024,1024]{1,0:T(8,128)(2,1)}) %all-reduce.19.cloned.1.call-update) | async-done | bytes 2097168 | tf_op jit(solution)/shard_map/psum | solution.py:217
  437.0 5.0 multiply_reduce_fusion.4
  442.9 2.5 fusion.115
  449.6 2.3 copy.63
  452.7 33.1 %while.61 = (s32[]{:T(128)}, f32[1024,4,64]{0,2,1:T(8,128)S(1)}, f32[1024,4,64]{0,2,1:T(8,128)}, bf16[2,512,256]{2,1,0:T(8,128)(2,1)}, bf16[2,512,4,64]{1,3,2,0:...) while((s32[]{:T(128)}, f32[1024,4,64]{0,2,1:T(8,128)S(1)}, ...), condition=%wide.region_30.31_spmd.clone.clone, body=%wide.region_28.30_spmd.clone.clone.sunk | while | flops 1376255488 | bytes 75299024 | solution.py:113
  456.4 3.6 fusion.264
  460.0 3.2 multiply_reduce_fusion.14
  463.1 2.4 multiply_convert_fusion.6
  472.4 4.6 fusion.264
  477.0 3.2 multiply_reduce_fusion.14
  480.2 2.4 multiply_convert_fusion.6
  493.4 3.2 fusion.103
  496.6 3.7 fusion.104
  508.9 36.7 %all-reduce = (bf16[1024]{0:T(1024)(128)(2,1)S(1)}, bf16[1024]{0:T(1024)(128)(2,1)S(1)}, bf16[1024]{0:T(1024)(128)(2,1)S(1)}, bf16[1024]{0:T(1024)(128)(2,1)S(1)...) all-reduce(bf16[1024]{0:T(1024)(128)(2,1)S(1)} %get-tuple-element.5, ...), channel_id=1, replica_groups=mesh['dp'=8,'tensor'=4] {'dp'}, use_global_device_ids=true, to_apply=%region_38.39 | all-reduce | flops 6144 | bytes 24576 | tf_op jit(solution)/shard_map/psum | solution.py:244
  549.2 28.9 %all-reduce.23.cloned.1.call-done = (bf16[1024,1024]{1,0:T(8,128)(2,1)}, bf16[1024,1024]{1,0:T(8,128)(2,1)}) async-done(((bf16[1024,1024]{1,0:T(8,128)(2,1)}, bf16[1024,1024]{1,0:T(8,128)(2,1)}), (bf16[1024,1024]{1,0:T(8,128)(2,1)}, bf16[1024,1024]{1,0:T(8,128)(2,1)})) %all-reduce.23.cloned.1.call-update) | async-done | bytes 4194320 | tf_op jit(solution)/shard_map/psum | solution.py:236
  578.1 4.2 convert_element_type.360
  582.4 2.5 convert_add_fusion
  584.9 271.7 %all-reduce.21.cloned.1.call-done = (bf16[1024,256]{0,1:T(8,128)(2,1)}, bf16[1024,256]{0,1:T(8,128)(2,1)}, bf16[1024,256]{0,1:T(8,128)(2,1)}, bf16[1024,256]{0,1...) async-done(((bf16[1024,256]{0,1:T(8,128)(2,1)}, ...) | async-done | bytes 8388624 | tf_op jit(solution)/shard_map/psum | solution.py:240
  856.6 2.3 copy.65
  858.9 2.3 copy.66
  861.2 2.3 copy.67
  869.1 4.2 convert_element_type.391
  873.3 2.5 convert_element_type.393
  (319 shorter events, 112.4 us)
Async XLA Ops:
  7.2 182.1 %copy-start = (bf16[1024,1024]{1,0:T(8,128)(2,1)S(1)}, bf16[1024,1024]{1,0:T(8,128)(2,1)}, u32[]{:S(2)}) copy-start(bf16[1024,1024]{1,0:T(8,128)(2,1)} %param.45) | copy-start | bytes 6291460
  7.2 92.7 %all-reduce.11.cloned.1.call-start = ((), (), s32[]{:S(2)}) async-start(), calls=%async_computation | async-start | bytes 4194304 | tf_op jit(solution)/shard_map/psum | solution.py:164
  7.3 6.2 copy-start.48
  42.1 6.2 copy-start.2
  42.1 6.2 copy-start.59
  42.1 6.2 copy-start.80
  45.6 139.3 %all-reduce.13.cloned.1.call-start = ((), (), s32[]{:S(2)}) async-start(), calls=%async_computation.1 | async-start | bytes 4194304 | tf_op jit(solution)/shard_map/psum | solution.py:177
  51.6 53.3 %copy-start.65 = (f32[1024]{0:T(1024)S(1)}, f32[1024]{0:T(1024)}, u32[]{:S(2)}) copy-start(f32[1024]{0:T(1024)} %param.37) | copy-start | bytes 12292
  51.6 53.3 %copy-start.71 = (f32[1024]{0:T(1024)S(1)}, f32[1024]{0:T(1024)}, u32[]{:S(2)}) copy-start(f32[1024]{0:T(1024)} %param.38) | copy-start | bytes 12292
  99.9 3.5 copy-start.12
  103.3 81.5 %copy-start.61 = (f32[1024]{0:T(1024)}, f32[1024]{0:T(1024)S(1)}, u32[]{:S(2)}) copy-start(f32[1024]{0:T(1024)S(1)} %broadcast_multiply_fusion.2) | copy-start | bytes 12292
  104.9 80.0 %copy-start.63 = (f32[1024]{0:T(1024)}, f32[1024]{0:T(1024)S(1)}, u32[]{:S(2)}) copy-start(f32[1024]{0:T(1024)S(1)} %fusion.106) | copy-start | bytes 12292
  133.3 125.8 %all-reduce.15.cloned.1.call-start = ((), (), s32[]{:S(2)}) async-start(), calls=%async_computation.2 | async-start | bytes 4194304 | tf_op jit(solution)/shard_map/psum | solution.py:185
  188.7 13.8 %copy-start.4 = (f32[1024,1024]{1,0:T(8,128)}, f32[1024,1024]{1,0:T(8,128)S(1)}, u32[]{:S(2)}) copy-start(f32[1024,1024]{1,0:T(8,128)S(1)} %get-tuple-element.626) | copy-start | bytes 12582916
  189.5 14.3 %copy-start.78 = (bf16[1024,1024]{1,0:T(8,128)(2,1)S(1)}, bf16[1024,1024]{1,0:T(8,128)(2,1)}, u32[]{:S(2)}) copy-start(bf16[1024,1024]{1,0:T(8,128)(2,1)} %param.46) | copy-start | bytes 6291460
  207.5 125.9 %all-reduce.17.cloned.1.call-start = ((), (), s32[]{:S(2)}) async-start(), calls=%async_computation.3 | async-start | bytes 4194304 | tf_op jit(solution)/shard_map/psum | solution.py:199
  263.4 3.8 copy-start.76
  267.2 5.6 copy-start.83
  270.6 6.0 copy-start.15
  281.8 6.8 copy-start.85
  281.8 155.2 %all-reduce.19.cloned.1.call-start = ((), (), s32[]{:S(2)}) async-start(), calls=%async_computation.4 | async-start | bytes 4194304 | tf_op jit(solution)/shard_map/psum | solution.py:217
  281.8 6.8 copy-start.5
  333.4 6.0 copy-start.6
  333.4 6.5 copy-start.16
  333.4 7.1 copy-start.28
  340.5 4.1 copy-start.56
  344.6 5.2 copy-start.11
  344.6 5.2 copy-start.26
  380.3 8.0 copy-start.38
  380.4 5.3 copy-start.35
  381.9 7.3 copy-start.32
  385.4 192.8 %all-reduce.23.cloned.1.call-start = ((), (), s32[]{:S(2)}) async-start(), calls=%async_computation.6 | async-start | bytes 8388608 | tf_op jit(solution)/shard_map/psum | solution.py:236
  389.1 47.9 %copy-start.8 = (bf16[1024,1024]{1,0:T(8,128)(2,1)S(1)}, bf16[1024,1024]{1,0:T(8,128)(2,1)}, u32[]{:S(2)}) copy-start(bf16[1024,1024]{1,0:T(8,128)(2,1)} %param.29) | copy-start | bytes 6291460
  389.1 47.9 %copy-start.62 = (f32[1024]{0:T(1024)S(1)}, f32[1024]{0:T(1024)}, u32[]{:S(2)}) copy-start(f32[1024]{0:T(1024)} %copy-done.61) | copy-start | bytes 12292
  389.2 47.8 %copy-start.64 = (f32[1024]{0:T(1024)S(1)}, f32[1024]{0:T(1024)}, u32[]{:S(2)}) copy-start(f32[1024]{0:T(1024)} %copy-done.63) | copy-start | bytes 12292
  389.2 47.8 %copy-start.66 = (f32[1024]{0:T(1024)S(1)}, f32[1024]{0:T(1024)}, u32[]{:S(2)}) copy-start(f32[1024]{0:T(1024)} %param.37) | copy-start | bytes 12292
  391.5 50.6 %copy-start.68 = (f32[1024]{0:T(1024)S(1)}, f32[1024]{0:T(1024)}, u32[]{:S(2)}) copy-start(f32[1024]{0:T(1024)} %copy-done.67) | copy-start | bytes 12292
  437.0 5.1 copy-start.13
  437.0 5.3 copy-start.18
  437.0 5.9 copy-start.29
  442.9 4.5 copy-start.58
  447.4 5.3 copy-start.3
  447.4 5.3 copy-start.10
  447.4 5.3 copy-start.14
  447.4 5.3 copy-start.24
  447.4 5.3 copy-start.60
  447.4 5.3 copy-start.81
  485.8 3.7 copy-start.31
  485.8 3.7 copy-start.49
  485.9 4.3 copy-start.40
  492.4 4.3 copy-start.33
  492.4 364.2 %all-reduce.21.cloned.1.call-start = ((), (), s32[]{:S(2)}) async-start(), calls=%async_computation.5 | async-start | bytes 16777216 | tf_op jit(solution)/shard_map/psum | solution.py:240
  493.4 6.9 copy-start.19
  493.4 6.9 copy-start.45
  496.6 5.3 copy-start.9
  578.1 4.2 copy-start.22
  578.1 4.2 copy-start.36
  856.6 6.9 copy-start.55
  856.6 8.1 copy-start.54
  856.6 9.2 %copy-start.53 = (bf16[256,1024]{1,0:T(8,128)(2,1)S(1)}, bf16[256,1024]{1,0:T(8,128)(2,1)}, u32[]{:S(2)}) copy-start(bf16[256,1024]{1,0:T(8,128)(2,1)} %get-tuple-element.608) | copy-start | bytes 1572868
  858.9 8.0 copy-start.52
  861.2 6.8 copy-start.51
  868.0 5.3 copy-start.37
  869.1 6.7 copy-start.1
  (33 other events, 62.7 us)
Sparse Core Ops, SparseCore 0:
  45.7 54.0 all-reduce.10
  133.4 51.4 all-reduce.12
  207.6 51.4 all-reduce.14
  281.9 51.4 all-reduce.16
  385.5 51.4 all-reduce.18
  492.5 85.5 all-reduce.22
  585.6 270.9 all-reduce.20
where the time goes:
time: 890 us; the launch traced here: 883 us
  waiting for transfers between devices  537 us (60%)
  matrix products  151 us (17%)
  other arithmetic  86.2 us (10%)
  local copies, waits for them, and re-layouts  53.8 us (6%)
  blocking collectives  36.7 us (4%)
  between operations  16 us (2%)
    psum x1, waiting for transfers between devices, shards(): lax.psum(grad_self_query.astype(jnp.bfloat16), 'dp').astype(jnp.float32)  272 us
    psum x1, waiting for transfers between devices, shards(): lax.psum(product(cross_mixed, cross_output).astype(jnp.bfloat16), 'tensor')  51.1 us
    psum x1, waiting for transfers between devices, shards(): lax.psum(product(hidden, feed_out).astype(jnp.bfloat16), 'tensor')  50.9 us
    psum x1, waiting for transfers between devices, shards(): lax.psum(product(self_mixed, self_output).astype(jnp.bfloat16), 'tensor')  48.3 us
    psum x1, waiting for transfers between devices, shards(): lax.psum(first_term.astype(jnp.bfloat16), 'tensor').astype(jnp.float32)  45.5 us
    psum x1, waiting for transfers between devices, shards(): lax.psum(transposed_right(grad_pre, feed_in).astype(jnp.bfloat16), 'tensor')  40.7 us
    dot_general x10, matrix products, product(): return jnp.dot(left, right, preferred_element_type=jnp.float32)  37.8 us
    psum x1, blocking collectives, shards(): lax.psum(grad_self_gain.astype(jnp.bfloat16), 'dp').astype(jnp.float32)  36.7 us
  transfers between devices with their start and end apart: 7, of which 7 were waited for; matrix products, arithmetic and copies ran while one was open for 5% of the time, Pallas kernels for 0%

commit v1 on v0

v1 whole, which is shorter than its diff:
```python
import jax
import jax.numpy as jnp
from jax import lax
from jax.experimental import pallas as pl
from jax.experimental.pallas import tpu as pltpu
from jax.sharding import PartitionSpec as P

BF = jnp.bfloat16
F32 = jnp.float32
HD = 64
CHUNKS = 4
EPSILON = 1e-05
NEGATIVE = -1e30
MESH = pl.DeviceIdType.MESH
STAGES = 7


def mm(a, b):
    return lax.dot_general(a, b, (((1,), (0,)), ((), ())), preferred_element_type=F32)


def mt(a, b):
    return lax.dot_general(a, b, (((1,), (1,)), ((), ())), preferred_element_type=F32)


def tm(a, b):
    return lax.dot_general(a, b, (((0,), (0,)), ((), ())), preferred_element_type=F32)


def layout(rows, slots, width, inner, hidden):
    heads = inner // HD
    chunk = rows // CHUNKS
    half, own = chunk // 2, chunk // 4
    v = pltpu.VMEM
    return dict(
        tok=v((rows, width), BF),
        mem=v((slots, width), BF),
        cot=v((CHUNKS, own, width), BF),
        wq=v((width, inner), BF),
        wk=v((width, inner), BF),
        wv=v((width, inner), BF),
        wo=v((inner, width), BF),
        cwq=v((width, inner), BF),
        cwk=v((width, inner), BF),
        cwv=v((width, inner), BF),
        cwo=v((inner, width), BF),
        win=v((width, hidden), BF),
        wout=v((hidden, width), BF),
        q=v((rows, inner), BF),
        k=v((rows, inner), BF),
        v=v((rows, inner), BF),
        kt=v((heads, HD, rows), BF),
        vt=v((heads, HD + 16, rows), BF),
        cq=v((rows, inner), BF),
        ck=v((slots, inner), BF),
        cv=v((slots, inner), BF),
        ckt=v((heads, HD, slots), BF),
        cvt=v((heads, HD + 16, slots), BF),
        mixed=v((rows, inner), BF),
        cmixed=v((rows, inner), BF),
        lse=v((CHUNKS, heads, 1, chunk), F32),
        clse=v((CHUNKS, heads, 1, chunk), F32),
        delta=v((heads, 1, chunk), F32),
        flat=v((inner, chunk), F32),
        dout=v((chunk, inner), BF),
        dk=v((rows, inner), F32),
        dv=v((rows, inner), F32),
        hid=v((rows, hidden), BF),
        slope=v((rows, hidden), BF),
        low0=v((rows, width), BF),
        low1=v((rows, width), BF),
        low2=v((rows, width), BF),
        low3=v((rows, width), BF),
        low4=v((rows, width), BF),
        outs=v((rows, width), BF),
        res=v((CHUNKS, own, width), F32),
        xh1=v((CHUNKS, own, width), F32),
        xh2=v((CHUNKS, own, width), F32),
        rs1=v((CHUNKS, own, 1), F32),
        rs2=v((CHUNKS, own, 1), F32),
        part=v((CHUNKS, chunk, width), BF),
        rc=v((CHUNKS, half, width), BF),
        ys=v((CHUNKS, half, width), BF),
        ry=v((CHUNKS, own, width), BF),
        vacc=v((8, 8, width), F32),
        gbuf=v((2 * hidden + 2 * width, width), BF),
        insem=pltpu.SemaphoreType.DMA((16,)),
        cotsem=pltpu.SemaphoreType.DMA((CHUNKS,)),
        osem=pltpu.SemaphoreType.DMA((4,)),
        ssem=pltpu.SemaphoreType.DMA((8, CHUNKS)),
        rsem=pltpu.SemaphoreType.DMA((8, CHUNKS)),
    )


INPUTS = (
    "tok", "wk", "wv", "wq", "wo", "mem", "cwk", "cwv", "cwq", "cwo",
    "win", "wout",
)


def layer_kernel(names, lens, vec, *refs):
    n_in = len(INPUTS)
    srcs = dict(zip(INPUTS, refs[:n_in]))
    cot_h = refs[n_in]
    out_h, tg_h, mg_h, g_h, vg_h = refs[n_in + 1:n_in + 6]
    S = dict(zip(names, refs[n_in + 6:]))

    rows, width = S["tok"].shape
    slots = S["mem"].shape[0]
    inner = S["wq"].shape[1]
    hidden = S["win"].shape[1]
    heads = inner // HD
    R = rows // CHUNKS
    HF, Q = R // 2, R // 4
    scale = HD ** -0.5
    t = lax.axis_index("tensor")
    yy = t // 2
    kk = t % 2
    core = {"tensor": t + 1 - 2 * kk}
    ypar = {"tensor": t + 2 - 4 * yy}

    def row(c):
        return pl.ds(pl.multiple_of(c * R, R), R)

    def own_rows(c):
        return pl.ds(pl.multiple_of(c * R + kk * HF + yy * Q, Q), Q)

    def y_rows(c):
        return pl.ds(pl.multiple_of(c * R + kk * HF + (1 - yy) * Q, Q), Q)

    loads = {n: pltpu.make_async_copy(srcs[n], S[n], S["insem"].at[j])
             for j, n in enumerate(INPUTS)}
    cots = [pltpu.make_async_copy(cot_h.at[own_rows(c)], S["cot"].at[c], S["cotsem"].at[c])
            for c in range(CHUNKS)]
    for n in INPUTS:
        loads[n].start()
    for c in cots:
        c.start()

    barrier = pltpu.get_barrier_semaphore()
    for peer in (core, ypar):
        pl.semaphore_signal(barrier, inc=1, device_id=peer, device_id_type=MESH)

    S["vt"][:, HD:, :] = jnp.ones((heads, 16, rows), BF)
    S["cvt"][:, HD:, :] = jnp.ones((heads, 16, slots), BF)
    S["vacc"][...] = jnp.zeros(S["vacc"].shape, F32)

    def wait_for(*which):
        for n in which:
            loads[n].wait()

    def project(src, wk, wv, kd, vd, ktd, vtd, count):
        def body(i, carry):
            r = row(i)
            x = src[r, :]
            kf = mm(x, wk[...])
            kd[r, :] = kf.astype(BF)
            kt = kf.T.astype(BF)
            vf = mm(x, wv[...])
            vd[r, :] = vf.astype(BF)
            vtt = vf.T.astype(BF)
            for h in range(heads):
                ktd[h, :, r] = kt[h * HD:(h + 1) * HD, :]
                vtd[h, :HD, r] = vtt[h * HD:(h + 1) * HD, :]
            return carry
        lax.fori_loop(0, count, body, 0)

    def project_q(src, w, dst):
        def body(i, carry):
            dst[row(i), :] = mm(src[row(i), :], w[...]).astype(BF)
            return carry
        lax.fori_loop(0, CHUNKS, body, 0)

    def lanes(h):
        return pl.ds(pl.multiple_of((h // 2) * 2 * HD, 2 * HD), 2 * HD)

    def pick(x, h):
        lane = lax.broadcasted_iota(jnp.int32, x.shape, 1) // HD
        return jnp.where(lane == h % 2, x, jnp.zeros_like(x))

    def masked(scores, c, causal, length):
        kid = lax.broadcasted_iota(jnp.int32, scores.shape, 0)
        ok = kid < length
        if causal:
            qid = c * R + lax.broadcasted_iota(jnp.int32, scores.shape, 1)
            ok = ok & (kid <= qid)
        return jnp.where(ok, scores * scale, NEGATIVE)

    def head_forward(h, c, q, k, vt, lse, causal, length):
        qm = pick(q[row(c), lanes(h)], h)
        s = masked(mt(k[:, lanes(h)], qm), c, causal, length)
        top = jnp.max(s, axis=0, keepdims=True)
        p = jnp.exp(s - top).astype(BF)
        o = mm(vt[h], p)
        total = o[HD:HD + 1, :]
        S["flat"][pl.ds(pl.multiple_of(h * HD, HD), HD), :] = o[:HD, :] / total
        lse[c, h] = top + jnp.log(total)

    def head_backward(h, c, q, k, v, kt, lse, causal, length):
        qm = pick(q[row(c), lanes(h)], h)
        s = masked(mt(k[:, lanes(h)], qm), c, causal, length)
        p = jnp.exp(s - lse[c, h])
        dom = pick(S["dout"][:, lanes(h)], h)
        dp = mt(v[:, lanes(h)], dom)
        S["dv"][:, lanes(h)] += mm(p.astype(BF), dom)
        ds = (p * (dp - S["delta"][h])).astype(BF)
        S["dk"][:, lanes(h)] += mm(ds, qm)
        S["flat"][pl.ds(pl.multiple_of(h * HD, HD), HD), :] = mm(kt[h], ds) * scale

    def unflatten():
        return S["flat"][...].T

    def wide(fn, dst, c):
        block = min(256, width)

        def body(j, carry):
            cols = pl.ds(pl.multiple_of(j * block, block), block)
            dst[c, :, cols] = fn(cols).astype(BF)
            return carry
        lax.fori_loop(0, width // block, body, 0)

    def set_delta(c, mixed, low, w):
        do = mt(low[row(c), :], w[...]).astype(BF)
        S["dout"][...] = do
        prod = do.astype(F32) * mixed[row(c), :].astype(F32)
        sel = (lax.broadcasted_iota(jnp.int32, (8, inner), 1) // HD
               == lax.broadcasted_iota(jnp.int32, (8, inner), 0)).astype(F32)
        d = lax.dot_general(sel, prod, (((1,), (1,)), ((), ())),
                            precision=lax.Precision.HIGHEST, preferred_element_type=F32)
        for h in range(heads):
            S["delta"][h] = d[h:h + 1, :]

    dec = lens[0]
    enc = lens[1]

    def each_head(fn, middle):
        def body(h, carry):
            @pl.when(h == heads // 2)
            def _():
                middle()
            fn(h)
            return carry
        lax.fori_loop(0, heads, body, 0)

    def compute(s, c, middle):
        part = S["part"]
        if s == 0:
            each_head(lambda h: head_forward(h, c, S["q"], S["k"], S["vt"], S["lse"], True, dec), middle)
            S["mixed"][row(c), :] = unflatten().astype(BF)
            wide(lambda n: mm(S["mixed"][row(c), :], S["wo"][:, n]), part, c)
        elif s == 1:
            S["cq"][row(c), :] = mm(S["low0"][row(c), :], S["cwq"][...]).astype(BF)
            each_head(lambda h: head_forward(h, c, S["cq"], S["ck"], S["cvt"], S["clse"], False, enc), middle)
            S["cmixed"][row(c), :] = unflatten().astype(BF)
            wide(lambda n: mm(S["cmixed"][row(c), :], S["cwo"][:, n]), part, c)
        elif s == 2:
            block = min(256, hidden)

            def body(j, carry):
                n = pl.ds(pl.multiple_of(j * block, block), block)
                v = mm(S["low1"][row(c), :], S["win"][:, n])
                cdf = 0.5 * (1.0 + lax.erf(v * 0.7071067811865476))
                S["hid"][row(c), n] = (v * cdf).astype(BF)
                S["slope"][row(c), n] = (
                    cdf + v * jnp.exp(-0.5 * v * v) * 0.3989422804014327).astype(BF)
                return carry
            lax.fori_loop(0, hidden // block, body, 0)
            middle()
            wide(lambda n: mm(S["hid"][row(c), :], S["wout"][:, n]), part, c)
        elif s == 3:
            block = min(256, hidden)

            def body(j, carry):
                n = pl.ds(pl.multiple_of(j * block, block), block)
                g = mt(S["low2"][row(c), :], S["wout"][n, :])
                S["slope"][row(c), n] = (g * S["slope"][row(c), n].astype(F32)).astype(BF)
                return carry
            lax.fori_loop(0, hidden // block, body, 0)
            middle()
            wide(lambda n: mt(S["slope"][row(c), :], S["win"][n, :]), part, c)
        elif s == 4:
            set_delta(c, S["cmixed"], S["low3"], S["cwo"])
            each_head(lambda h: head_backward(h, c, S["cq"], S["ck"], S["cv"], S["ckt"], S["clse"], False, enc), middle)
            S["cq"][row(c), :] = unflatten().astype(BF)
            wide(lambda n: mt(S["cq"][row(c), :], S["cwq"][n, :]), part, c)
        elif s == 5:
            set_delta(c, S["mixed"], S["low4"], S["wo"])
            each_head(lambda h: head_backward(h, c, S["q"], S["k"], S["v"], S["kt"], S["lse"], True, dec), middle)
            S["q"][row(c), :] = unflatten().astype(BF)
            S["k"][row(c), :] = (S["dk"][row(c), :] * scale).astype(BF)
            S["v"][row(c), :] = S["dv"][row(c), :].astype(BF)
            wide(lambda n: mt(S["q"][row(c), :], S["wq"][n, :])
                 + mt(S["k"][row(c), :], S["wk"][n, :])
                 + mt(S["v"][row(c), :], S["wv"][n, :]), part, c)
        else:
            middle()
            wide(lambda n: mt(S["ck"][row(c), :], S["cwk"][n, :])
                 + mt(S["cv"][row(c), :], S["cwv"][n, :]), part, c)

    lows = [S["low0"], S["low1"], S["low2"], S["low3"], S["low4"], S["low1"], S["low2"]]

    def remote(src, dst, phase, c, peer):
        return pltpu.make_async_remote_copy(
            src_ref=src, dst_ref=dst, send_sem=S["ssem"].at[phase, c],
            recv_sem=S["rsem"].at[phase, c], device_id=peer, device_id_type=MESH)

    def core_part(c):
        theirs = pl.ds(pl.multiple_of((1 - kk) * HF, HF), HF)
        return remote(S["part"].at[c, theirs], S["rc"].at[c], 0, c, core)

    def y_part(c):
        theirs = pl.ds(pl.multiple_of((1 - yy) * Q, Q), Q)
        return remote(S["ys"].at[c, theirs], S["ry"].at[c], 1, c, ypar)

    def gather(buf, c, which, base):
        r = y_rows(c) if which == 2 else own_rows(c)
        return remote(buf.at[r], buf.at[r], base + which, c, ypar if which == 0 else core)

    def p0(c):
        core_part(c).start()

    def p1(c):
        core_part(c).wait()
        step = min(32, HF)

        def body(j, carry):
            r = pl.ds(pl.multiple_of(j * step, step), step)
            m = pl.ds(pl.multiple_of(kk * HF + j * step, step), step)
            S["ys"][c, r, :] = (S["part"][c, m, :].astype(F32)
                                + S["rc"][c, r, :].astype(F32)).astype(BF)
            return carry
        lax.fori_loop(0, HF // step, body, 0)
        y_part(c).start()

    def mean(x):
        return jnp.sum(x, axis=-1, keepdims=True) * (1.0 / width)

    def norm(x, j):
        center = x - mean(x)
        inv = lax.rsqrt(mean(center * center) + EPSILON)
        xhat = center * inv
        return xhat, inv, xhat * vec[2 * j:2 * j + 1, :] + vec[2 * j + 1:2 * j + 2, :]

    def fold(x):
        return jnp.sum(x.reshape(x.shape[0] // 8, 8, width), axis=0)

    def norm_back(e, xhat, inv, j):
        S["vacc"][2 * j] += fold(e * xhat)
        S["vacc"][2 * j + 1] += fold(e)
        eg = e * vec[2 * j:2 * j + 1, :]
        return (eg - mean(eg) - xhat * mean(eg * xhat)) * inv

    def p2(s, c):
        y_part(c).wait()
        if s == 2:
            @pl.when(c == CHUNKS - 1)
            def _():
                for x in cots:
                    x.wait()
        step = min(16, Q)
        buf = lows[s]

        def body(j, carry):
            r = pl.ds(pl.multiple_of(j * step, step), step)
            m = pl.ds(pl.multiple_of(yy * Q + j * step, step), step)
            o = pl.ds(pl.multiple_of(c * R + kk * HF + yy * Q + j * step, step), step)
            x = S["ys"][c, m, :].astype(F32) + S["ry"][c, r, :].astype(F32)
            if s == 0:
                xhat, inv, y = norm(S["tok"][o, :].astype(F32) + x, 0)
                S["xh1"][c, r, :] = xhat
                S["rs1"][c, r, :] = inv
                S["res"][c, r, :] = y
            elif s == 1:
                xhat, inv, y = norm(S["res"][c, r, :] + x, 1)
                S["xh2"][c, r, :] = xhat
                S["rs2"][c, r, :] = inv
                S["res"][c, r, :] = y
            elif s == 2:
                xhat, inv, y = norm(S["res"][c, r, :] + x, 2)
                S["outs"][o, :] = y.astype(BF)
                rid = (c * R + kk * HF + yy * Q + j * step
                       + lax.broadcasted_iota(jnp.int32, (step, width), 0))
                seed = jnp.where(rid < dec, S["cot"][c, r, :].astype(F32), 0.0)
                y = norm_back(seed, xhat, inv, 2)
                S["res"][c, r, :] = y
            elif s == 3:
                y = norm_back(S["res"][c, r, :] + x, S["xh2"][c, r, :], S["rs2"][c, r, :], 1)
                S["res"][c, r, :] = y
            elif s == 4:
                y = norm_back(S["res"][c, r, :] + x, S["xh1"][c, r, :], S["rs1"][c, r, :], 0)
                S["res"][c, r, :] = y
            elif s == 5:
                y = S["res"][c, r, :] + x
            else:
                y = x
            buf[o, :] = y.astype(BF)
            return carry
        lax.fori_loop(0, Q // step, body, 0)
        gather(buf, c, 0, 2).start()
        gather(buf, c, 1, 2).start()
        if s == 2:
            gather(S["outs"], c, 0, 5).start()
            gather(S["outs"], c, 1, 5).start()

    def p3(s, c):
        sets = ((lows[s], 2), (S["outs"], 5)) if s == 2 else ((lows[s], 2),)
        for buf, base in sets:
            gather(buf, c, 0, base).wait()
            gather(buf, c, 2, base).start()

    def p4(s, c):
        sets = ((lows[s], 2), (S["outs"], 5)) if s == 2 else ((lows[s], 2),)
        for buf, base in sets:
            gather(buf, c, 1, base).wait()
            gather(buf, c, 2, base).wait()

    def grad_piece(g, i):
        if g == 0:
            n = pl.ds(pl.multiple_of(i * 256, 256), 256)
            S["gbuf"][pl.ds(pl.multiple_of(i * 256, 256), 256), :] = tm(
                S["hid"][:, n], S["low2"][...]).astype(BF)
        elif g == 1:
            n = pl.ds(pl.multiple_of(i * 256, 256), 256)
            S["gbuf"][pl.ds(pl.multiple_of(hidden + i * 256, 256), 256), :] = tm(
                S["low1"][:, n], S["slope"][...]).astype(BF)
        else:
            n = pl.ds(pl.multiple_of(i * 256, 256), 256)
            r = pl.ds(pl.multiple_of(hidden + (g - 1) * width + i * 256, 256), 256)
            if g == 2:
                a, b, d = S["low0"], S["mem"], S["low3"]
                x, y, z, w = S["cq"], S["ck"], S["cv"], S["cmixed"]
            else:
                a, b, d = S["tok"], S["tok"], S["low4"]
                x, y, z, w = S["q"], S["k"], S["v"], S["mixed"]
            S["gbuf"][r, 0 * inner:1 * inner] = tm(a[:, n], x[...]).astype(BF)
            S["gbuf"][r, 1 * inner:2 * inner] = tm(b[:, n], y[...]).astype(BF)
            S["gbuf"][r, 2 * inner:3 * inner] = tm(b[:, n], z[...]).astype(BF)
            S["gbuf"][r, 3 * inner:4 * inner] = tm(d[:, n], w[...]).astype(BF)

    wait_for("tok", "wk", "wv", "wq")
    project(S["tok"], S["wk"], S["wv"], S["k"], S["v"], S["kt"], S["vt"], CHUNKS)
    project_q(S["tok"], S["wq"], S["q"])
    pl.semaphore_wait(barrier, 2)
    wait_for("wo")

    def lagged(i, lag, fn, s):
        c = lax.rem(CHUNKS - 1 - i + lag, CHUNKS)

        @pl.when(i >= lag)
        def _():
            fn(s, c)
        if s > 0:
            @pl.when(i < lag)
            def _():
                fn(s - 1, c)

    for s in range(STAGES):
        if s == 1:
            wait_for("mem", "cwk", "cwv", "cwq", "cwo")
            project(S["mem"], S["cwk"], S["cwv"], S["ck"], S["cv"], S["ckt"], S["cvt"], CHUNKS)
        if s == 2:
            wait_for("win", "wout")
        if s in (4, 5):
            S["dk"][...] = jnp.zeros(S["dk"].shape, F32)
            S["dv"][...] = jnp.zeros(S["dv"].shape, F32)

        def slot(i, carry, s=s):
            c = CHUNKS - 1 - i
            if s > 0:
                p4(s - 1, c)

            def middle():
                lagged(i, 3, p3, s)
                lagged(i, 2, p2, s)
                if s > 0:
                    p1(lax.rem(c + 1, CHUNKS))
                else:
                    @pl.when(i >= 1)
                    def _():
                        p1(lax.rem(c + 1, CHUNKS))
            compute(s, c, middle)
            p0(c)
            if s == 4:
                grad_piece(0, i)
                grad_piece(1, i)
            elif s == 5:
                grad_piece(2, i)
            elif s == 6:
                grad_piece(3, i)
            return carry
        lax.fori_loop(0, CHUNKS, slot, 0)
        if s == 4:
            S["ck"][...] = (S["dk"][...] * scale).astype(BF)
            S["cv"][...] = S["dv"][...].astype(BF)

    last = STAGES - 1
    g_copy = pltpu.make_async_copy(S["gbuf"], g_h, S["osem"].at[0])
    g_copy.start()
    o_copy = pltpu.make_async_copy(S["outs"], out_h, S["osem"].at[1])
    o_copy.start()

    p1(0)
    p2(last, 1)
    p3(last, 2)
    p2(last, 0)
    p3(last, 1)
    p3(last, 0)
    for c in range(CHUNKS):
        p4(last, CHUNKS - 1 - c)
    t_copy = pltpu.make_async_copy(lows[5], tg_h, S["osem"].at[2])
    t_copy.start()
    m_copy = pltpu.make_async_copy(lows[6], mg_h, S["osem"].at[3])
    m_copy.start()
    vg_h[...] = jnp.sum(S["vacc"][...], axis=1)
    for x in (g_copy, o_copy, t_copy, m_copy):
        x.wait()


def shards(
    tokens, memory, decoder_length, memory_length,
    self_query, self_key, self_value, self_output, self_gain, self_bias,
    cross_query, cross_key, cross_value, cross_output, cross_gain, cross_bias,
    feed_in, feed_out, feed_gain, feed_bias, cotangent,
):
    rows, width = tokens.shape
    slots = memory.shape[0]
    inner = self_query.shape[1]
    hidden = feed_in.shape[1]
    lens = jnp.concatenate([decoder_length, memory_length])
    vec = jnp.stack([self_gain, self_bias, cross_gain, cross_bias, feed_gain, feed_bias,
                     feed_gain, feed_bias])
    scratch = layout(rows, slots, width, inner, hidden)
    names = tuple(scratch)
    given = dict(tok=tokens, mem=memory, wq=self_query, wk=self_key, wv=self_value,
                 wo=self_output, cwq=cross_query, cwk=cross_key, cwv=cross_value,
                 cwo=cross_output, win=feed_in, wout=feed_out)
    any_spec = pl.BlockSpec(memory_space=pl.ANY)
    total = 2 * hidden + 2 * width

    def kernel(*refs):
        layer_kernel(names, *refs)

    out, tg, mg, g, vg = pl.pallas_call(
        kernel,
        out_shape=(
            jax.ShapeDtypeStruct((rows, width), BF),
            jax.ShapeDtypeStruct((rows, width), BF),
            jax.ShapeDtypeStruct((slots, width), BF),
            jax.ShapeDtypeStruct((total, width), BF),
            jax.ShapeDtypeStruct((8, width), F32),
        ),
        in_specs=[pl.BlockSpec(memory_space=pltpu.SMEM), pl.BlockSpec(memory_space=pltpu.VMEM)]
        + [any_spec] * (len(INPUTS) + 1),
        out_specs=(any_spec,) * 4 + (pl.BlockSpec(memory_space=pltpu.VMEM),),
        scratch_shapes=list(scratch.values()),
        compiler_params=pltpu.CompilerParams(
            collective_id=0, has_side_effects=True, vmem_limit_bytes=67043328),
        name="layer",
    )(lens, vec, *[given[n] for n in INPUTS], cotangent)

    vecs = lax.psum(vg, ("dp", "tensor"))
    grads = lax.psum(g, "dp").astype(F32)

    def block(start):
        x = grads[start:start + width]
        return (x[:, :inner], x[:, inner:2 * inner], x[:, 2 * inner:3 * inner],
                x[:, 3 * inner:].T)

    cq, ck, cv, co = block(2 * hidden)
    sq, sk, sv, so = block(2 * hidden + width)
    return (
        out, tg.astype(F32), mg.astype(F32),
        sq, sk, sv, so, vecs[0], vecs[1],
        cq, ck, cv, co, vecs[2], vecs[3],
        grads[hidden:2 * hidden], grads[:hidden], vecs[4], vecs[5],
    )


def solution(mesh):
    rows = P("dp", None)
    tail = P(None, "tensor")
    head = P("tensor", None)
    whole = P()
    return jax.shard_map(
        shards,
        mesh=mesh,
        in_specs=(
            rows, rows, P("dp"), P("dp"),
            tail, tail, tail, head, whole, whole,
            tail, tail, tail, head, whole, whole,
            tail, head, whole, whole, rows,
        ),
        out_specs=(
            rows, rows, rows,
            tail, tail, tail, head, whole, whole,
            tail, tail, tail, head, whole, whole,
            tail, head, whole, whole,
        ),
        check_vma=False,
    )
```

time: 890 us -> 553 us (0.62)
  waiting for transfers between devices: 537 us -> 220 us
  Pallas kernels: 0 us -> 235 us
  matrix products: 151 us -> 0 us
  other arithmetic: 86.2 us -> 16.9 us
  local copies, waits for them, and re-layouts: 53.8 us -> 20.7 us
    psum x7 -> x1, waiting for transfers between devices: 537 us -> 220 us  [shards(): grads = lax.psum(g, 'dp').astype(F32)]
    pallas_call x0 -> x1, Pallas kernels: none -> 235 us  [shards(): pl.pallas_call(kernel, out_shape=(jax.ShapeDtypeStruct((rows, width), BF)...]
    dot_general x58 -> x0, matrix products: 151 us -> none  [the longest x10 37.8 us: product(): return jnp.dot(left, right, preferred_element_type=jnp.float32)]
    reduce_sum x16 -> x0, other arithmetic: 43 us -> none  [the longest x6 18.4 us: layer_norm(): center = summed - jnp.mean(summed, axis=-1, keepdims=True)]
    unnamed x177 -> x11, local copies, waits for them, and re-layouts: 33.8 us -> 5.49 us
    convert_element_type x22 -> x3, other arithmetic: 31.1 us -> 16.3 us  [the longest x1 11.3 us: shards(): grads = lax.psum(g, 'dp').astype(F32)]
    slice x0 -> x3, local copies, waits for them, and re-layouts: none -> 12.1 us  [the longest x1 6.81 us: shards(): grads[:hidden]]
  transfers between devices with their start and end apart: 7 -> 1, of which waited for: 7 -> 1; matrix products, arithmetic and copies ran while one was open for 5% -> 1% of each run, Pallas kernels for 0% -> 0%
where the time goes in v1:
time: 553 us; the launch traced here: 552 us
  Pallas kernels  235 us (42%)
  waiting for transfers between devices  220 us (40%)
  blocking collectives  44.7 us (8%)
  local copies, waits for them, and re-layouts  20.7 us (4%)
  other arithmetic  16.9 us (3%)
  between operations  15.4 us (3%)
    pallas_call x1, Pallas kernels, shards(): pl.pallas_call(kernel, out_shape=(jax.ShapeDtypeStruct((rows, width), BF)...  235 us
    psum x1, waiting for transfers between devices, shards(): grads = lax.psum(g, 'dp').astype(F32)  220 us
    psum x1, blocking collectives, shards(): vecs = lax.psum(vg, ('dp', 'tensor'))  44.7 us
    convert_element_type x1, other arithmetic, shards(): grads = lax.psum(g, 'dp').astype(F32)  11.3 us
  transfers between devices with their start and end apart: 1, of which 1 were waited for; matrix products, arithmetic and copies ran while one was open for 1% of the time, Pallas kernels for 0%

profile of v1, /device:TPU:0, one launch (start us, length us, event | category | flops | bytes accessed | tf_op | source)
XLA Modules:
  0.0 552.4 jit_solution(8778474555673657198)
XLA Ops:
  7.2 0.0 all-reduce.2.cloned.1.call-start
  8.5 0.6 pad_add_fusion.refs_0_
  9.1 1.5 stack.29.refs_1_
  10.6 234.8 %layer.1 = (bf16[1024,1024]{1,0:T(8,128)(2,1)}, bf16[1024,1024]{1,0:T(8,128)(2,1)}, bf16[1024,1024]{1,0:T(8,128)(2,1)}, bf16[4096,1024]{1,0:T(8,128)(2,1)}, f32[8,1024]{1,0:T(8,128)}) custom-call(s32[2]{0:T(128)} %pad_add_fusion.refs_0_, f32[8,1024]{1,0:T(8,128)} %stack.29.refs_1_, bf16[1024,1024]{1,0:T(8,128)(2,1)} %refs_2_.1, bf16[1024,256]{1,0:T(8,128)(2,1)} %refs_3_.1, ...), custom_call_target="tpu_custom_call" | custom-call | tf_op jit(solution)/shard_map/layer/pallas_call | solution.py:543
  245.4 0.0 copy-start.1
  245.4 0.0 all-reduce.2.cloned.1.call-update
  245.5 0.0 copy-start
  245.5 1.5 copy-done.1
  247.0 2.5 convert_element_type.10
  249.5 0.0 copy-start.3
  249.5 0.0 copy-done
  249.5 2.6 convert_element_type.9
  252.1 0.0 copy-done.3
  252.1 44.7 %psum.15 = f32[8,1024]{1,0:T(8,128)S(1)} all-reduce(f32[8,1024]{1,0:T(8,128)S(1)} %copy-done.3), channel_id=1, replica_groups=mesh['dp'=8,'tensor'=4] {'dp','tensor'}, use_global_device_ids=true, to_apply=%region_1.0 | all-reduce | flops 8192 | bytes 65536 | tf_op jit(solution)/shard_map/psum | solution.py:561
  296.8 0.6 fusion.2
  297.4 219.8 %all-reduce.2.cloned.1.call-done = bf16[4096,1024]{1,0:T(8,128)(2,1)} async-done(((bf16[4096,1024]{1,0:T(8,128)(2,1)}), bf16[4096,1024]{1,0:T(8,128)(2,1)}) %all-reduce.2.cloned.1.call-update) | async-done | bytes 8388624 | tf_op jit(solution)/shard_map/psum | solution.py:562
  517.2 11.3 %convert_element_type.11 = f32[4096,1024]{1,0:T(8,128)} convert(bf16[4096,1024]{1,0:T(8,128)(2,1)} %all-reduce.2.cloned.1.call-done) | non-fusion elementwise | flops 4194304 | bytes 25165824 | tf_op jit(solution)/shard_map/convert_element_type | solution.py:562
  528.5 1.7 slice_bitcast_fusion
  530.1 1.3 copy.40
  531.4 1.3 copy.41
  532.8 4.6 fusion.1
  537.4 0.0 copy-start.2
  537.4 6.8 %fusion = (f32[1024,1024]{1,0:T(8,128)}, f32[1024,1024]{1,0:T(8,128)}) fusion(bf16[4096,1024]{1,0:T(8,128)(2,1)} %all-reduce.2.cloned.1.call-done), kind=kLoop, calls=%fused_computation.3 | loop fusion | bytes 16777216 | tf_op jit(solution)/shard_map/slice | solution.py:575
  544.2 0.0 copy-done.2
  544.2 1.3 copy.46
Async XLA Ops:
  7.2 510.0 %all-reduce.2.cloned.1.call-start = ((), (), s32[]{:S(2)}) async-start(), calls=%async_computation | async-start | bytes 16777216 | tf_op jit(solution)/shard_map/psum | solution.py:562
  245.4 1.6 copy-start.1
  245.5 4.0 copy-start
  249.5 2.6 copy-start.3
  537.4 6.8 %copy-start.2 = (bf16[1024,1024]{1,0:T(8,128)(2,1)S(1)}, bf16[1024,1024]{1,0:T(8,128)(2,1)}, u32[]{:S(2)}) copy-start(bf16[1024,1024]{1,0:T(8,128)(2,1)} %get-tuple-element.83) | copy-start | bytes 6291460
Sparse Core Ops, SparseCore 0:
  245.6 271.5 all-reduce.1

commit v2 on v1

--- a/solution.py
+++ b/solution.py
@@ -27,7 +27,22 @@
     return lax.dot_general(a, b, (((0,), (0,)), ((), ())), preferred_element_type=F32)
 
 
-def layout(rows, slots, width, inner, hidden):
+PIECE = 256
+RING = 8
+
+
+def split_sizes(copies):
+    sizes, rows = [], PIECE
+    for _ in range(copies.bit_length() - 1):
+        halve = rows // 2 >= 16
+        rows = rows // 2 if halve else rows
+        sizes.append((rows, halve))
+    return sizes
+
+
+def layout(rows, slots, width, inner, hidden, copies):
+    sizes = split_sizes(copies)
+    pieces = (2 * hidden + 2 * width) // PIECE
     heads = inner // HD
     chunk = rows // CHUNKS
     half, own = chunk // 2, chunk // 4
@@ -84,6 +99,16 @@
         ry=v((CHUNKS, own, width), BF),
         vacc=v((8, 8, width), F32),
         gbuf=v((2 * hidden + 2 * width, width), BF),
+        vsum=v((8, width), F32),
+        vrec=v((len(sizes) + 2, 8, width), F32),
+        **{f"dr{j}": v((RING, n, width), BF) for j, (n, _) in enumerate(sizes)},
+        ag=v((RING, [n for n, h in sizes if h][-1], width), BF),
+        freed=pltpu.SemaphoreType.REGULAR((len(sizes), RING)),
+        dssem=pltpu.SemaphoreType.DMA((2 * len(sizes), RING)),
+        drsem=pltpu.SemaphoreType.DMA((2 * len(sizes), RING)),
+        gsem=pltpu.SemaphoreType.DMA((4, pieces)),
+        vssem=pltpu.SemaphoreType.DMA((len(sizes) + 2,)),
+        vrsem=pltpu.SemaphoreType.DMA((len(sizes) + 2,)),
         insem=pltpu.SemaphoreType.DMA((16,)),
         cotsem=pltpu.SemaphoreType.DMA((CHUNKS,)),
         osem=pltpu.SemaphoreType.DMA((4,)),
@@ -98,12 +123,12 @@
 )
 
 
-def layer_kernel(names, lens, vec, *refs):
+def layer_kernel(names, copies, lens, vec, *refs):
     n_in = len(INPUTS)
     srcs = dict(zip(INPUTS, refs[:n_in]))
     cot_h = refs[n_in]
-    out_h, tg_h, mg_h, g_h, vg_h = refs[n_in + 1:n_in + 6]
-    S = dict(zip(names, refs[n_in + 6:]))
+    out_h, tg_h, mg_h, gf_h, gq_h, go_h, vg_h = refs[n_in + 1:n_in + 8]
+    S = dict(zip(names, refs[n_in + 8:]))
 
     rows, width = S["tok"].shape
     slots = S["mem"].shape[0]
@@ -119,6 +144,17 @@
     core = {"tensor": t + 1 - 2 * kk}
     ypar = {"tensor": t + 2 - 4 * yy}
 
+    me = lax.axis_index("dp")
+    sizes = split_sizes(copies)
+    bits = len(sizes)
+    pieces = (2 * hidden + 2 * width) // PIECE
+
+    def side(weight):
+        return lax.rem(lax.div(me, weight), 2)
+
+    def dp_peer(weight):
+        return {"dp": me + weight * (1 - 2 * side(weight))}
+
     def row(c):
         return pl.ds(pl.multiple_of(c * R, R), R)
 
@@ -138,7 +174,7 @@
         c.start()
 
     barrier = pltpu.get_barrier_semaphore()
-    for peer in (core, ypar):
+    for peer in [core, ypar] + [dp_peer(1 << j) for j in range(bits)]:
         pl.semaphore_signal(barrier, inc=1, device_id=peer, device_id_type=MESH)
 
     S["vt"][:, HD:, :] = jnp.ones((heads, 16, rows), BF)
@@ -297,7 +333,7 @@
             wide(lambda n: mt(S["ck"][row(c), :], S["cwk"][n, :])
                  + mt(S["cv"][row(c), :], S["cwv"][n, :]), part, c)
 
-    lows = [S["low0"], S["low1"], S["low2"], S["low3"], S["low4"], S["low1"], S["low2"]]
+    lows = [S["low0"], S["low1"], S["low2"], S["low3"], S["low4"], S["low2"], S["low1"]]
 
     def remote(src, dst, phase, c, peer):
         return pltpu.make_async_remote_copy(
@@ -415,17 +451,13 @@
             gather(buf, c, 2, base).wait()
 
     def grad_piece(g, i):
+        n = pl.ds(pl.multiple_of(i * PIECE, PIECE), PIECE)
+        r = pl.ds(pl.multiple_of((g * CHUNKS + i) * PIECE, PIECE), PIECE)
         if g == 0:
-            n = pl.ds(pl.multiple_of(i * 256, 256), 256)
-            S["gbuf"][pl.ds(pl.multiple_of(i * 256, 256), 256), :] = tm(
-                S["hid"][:, n], S["low2"][...]).astype(BF)
+            S["gbuf"][r, :] = tm(S["hid"][:, n], S["low2"][...]).astype(BF)
         elif g == 1:
-            n = pl.ds(pl.multiple_of(i * 256, 256), 256)
-            S["gbuf"][pl.ds(pl.multiple_of(hidden + i * 256, 256), 256), :] = tm(
-                S["low1"][:, n], S["slope"][...]).astype(BF)
+            S["gbuf"][r, :] = tm(S["low1"][:, n], S["slope"][...]).astype(BF)
         else:
-            n = pl.ds(pl.multiple_of(i * 256, 256), 256)
-            r = pl.ds(pl.multiple_of(hidden + (g - 1) * width + i * 256, 256), 256)
             if g == 2:
                 a, b, d = S["low0"], S["mem"], S["low3"]
                 x, y, z, w = S["cq"], S["ck"], S["cv"], S["cmixed"]
@@ -435,12 +467,139 @@
             S["gbuf"][r, 0 * inner:1 * inner] = tm(a[:, n], x[...]).astype(BF)
             S["gbuf"][r, 1 * inner:2 * inner] = tm(b[:, n], y[...]).astype(BF)
             S["gbuf"][r, 2 * inner:3 * inner] = tm(b[:, n], z[...]).astype(BF)
-            S["gbuf"][r, 3 * inner:4 * inner] = tm(d[:, n], w[...]).astype(BF)
+            S["gbuf"][r, 3 * inner:4 * inner] = tm(w[...], d[:, n]).astype(BF)
+
+    def weight(step, p):
+        if bits < 2 or step > 1:
+            return 1 << step
+        swap = lax.div(lax.rem(p, 4), 3)
+        return 1 + swap if step == 0 else 2 - swap
+
+    def start_of(step, p):
+        at = p * PIECE
+        for j in range(step):
+            if sizes[j][1]:
+                at = at + side(weight(j, p)) * sizes[j][0]
+        return at
+
+    def piece_rows(at, n):
+        return pl.ds(pl.multiple_of(at, n), n)
+
+    def reduce_copy(step, p):
+        n, halve = sizes[step]
+        w = weight(step, p)
+        at = start_of(step, p)
+        if halve:
+            at = at + (1 - side(w)) * n
+        slot = lax.rem(p, RING)
+        return pltpu.make_async_remote_copy(
+            src_ref=S["gbuf"].at[piece_rows(at, n)], dst_ref=S[f"dr{step}"].at[slot],
+            send_sem=S["dssem"].at[step, slot], recv_sem=S["drsem"].at[step, slot],
+            device_id=dp_peer(w), device_id_type=MESH)
+
+    def reduce_add(step, p):
+        n, halve = sizes[step]
+        at = start_of(step + 1, p)
+        slot = lax.rem(p, RING)
+        block = min(32, n)
+
+        def body(j, carry):
+            r = pl.ds(pl.multiple_of(at + j * block, block), block)
+            m = pl.ds(pl.multiple_of(j * block, block), block)
+            S["gbuf"][r, :] = (S["gbuf"][r, :].astype(F32)
+                               + S[f"dr{step}"][slot, m, :].astype(F32)).astype(BF)
+            return carry
+        lax.fori_loop(0, n // block, body, 0)
+
+    halved = sum(1 for _, h in sizes if h)
+    steps = bits + halved
+
+    def gather_copy(step, p):
+        n, _ = sizes[step]
+        r = S["gbuf"].at[piece_rows(start_of(step + 1, p), n)]
+        slot = lax.rem(p, RING)
+        return pltpu.make_async_remote_copy(
+            src_ref=r, dst_ref=S["ag"].at[slot] if step == halved - 1 else r,
+            send_sem=S["dssem"].at[bits + step, slot], recv_sem=S["drsem"].at[bits + step, slot],
+            device_id=dp_peer(weight(step, p)), device_id_type=MESH)
+
+    def gather_end(step, p):
+        gather_copy(step, p).wait()
+        if step == halved - 1:
+            n, _ = sizes[step]
+            at = start_of(step, p) + (1 - side(weight(step, p))) * n
+            S["gbuf"][piece_rows(at, n), :] = S["ag"][lax.rem(p, RING)]
+
+    def gather_begin(step, p):
+        if step < halved - 1:
+            pl.semaphore_wait(S["freed"].at[step, lax.rem(p, RING)], 1)
+        gather_copy(step, p).start()
+
+    def result_copies(p, ff):
+        r = pl.ds(pl.multiple_of(p * PIECE, PIECE), PIECE)
+        if ff:
+            return [pltpu.make_async_copy(S["gbuf"].at[r], gf_h.at[r], S["gsem"].at[0, p])]
+        g = lax.div(p - 2 * CHUNKS, CHUNKS)
+        n = pl.ds(pl.multiple_of(lax.rem(p, CHUNKS) * PIECE, PIECE), PIECE)
+        block = [S["gbuf"].at[r, pl.ds(j * inner, inner)] for j in range(4)]
+        return [pltpu.make_async_copy(block[j], gq_h.at[g, j, n], S["gsem"].at[j, p])
+                for j in range(3)] + [
+            pltpu.make_async_copy(block[3], go_h.at[g, :, n], S["gsem"].at[3, p])]
+
+    def dp_step(k, p):
+        if 1 <= k <= bits:
+            reduce_copy(k - 1, p).wait()
+            if k < halved:
+                pl.semaphore_signal(S["freed"].at[k - 1, lax.rem(p, RING)], inc=1,
+                                    device_id=dp_peer(weight(k - 1, p)), device_id_type=MESH)
+            reduce_add(k - 1, p)
+        elif k > bits:
+            gather_end(halved - (k - bits), p)
+        if k < bits:
+            reduce_copy(k, p).start()
+        elif k < steps:
+            gather_begin(halved - 1 - (k - bits), p)
+        else:
+            @pl.when(p < 2 * CHUNKS)
+            def _():
+                for x in result_copies(p, True):
+                    x.start()
+
+            @pl.when(p >= 2 * CHUNKS)
+            def _():
+                for x in result_copies(p, False):
+                    x.start()
+
+    dp_order = [0] + [k for k in range(steps - 1, 1, -1)] + [steps, 1]
+
+    def dp_slot(j):
+        for k in dp_order:
+            p = j - k
+
+            @pl.when((p >= 0) & (p < pieces))
+            def _(k=k, p=p):
+                dp_step(k, p)
+
+    peers = [core, ypar] + [dp_peer(1 << j) for j in range(bits)]
+
+    def vec_copy(k):
+        return pltpu.make_async_remote_copy(
+            src_ref=S["vsum"], dst_ref=S["vrec"].at[k], send_sem=S["vssem"].at[k],
+            recv_sem=S["vrsem"].at[k], device_id=peers[k], device_id_type=MESH)
+
+    def vec_step(k):
+        if k == 0:
+            S["vsum"][...] = jnp.sum(S["vacc"][...], axis=1)
+        else:
+            vec_copy(k - 1).wait()
+            S["vsum"][...] += S["vrec"][k - 1]
+        if k < len(peers):
+            vec_copy(k).start()
 
     wait_for("tok", "wk", "wv", "wq")
     project(S["tok"], S["wk"], S["wv"], S["k"], S["v"], S["kt"], S["vt"], CHUNKS)
     project_q(S["tok"], S["wq"], S["q"])
-    pl.semaphore_wait(barrier, 2)
+    pl.semaphore_wait(barrier, 2 + bits)
     wait_for("wo")
 
     def lagged(i, lag, fn, s):
@@ -480,13 +639,14 @@
                         p1(lax.rem(c + 1, CHUNKS))
             compute(s, c, middle)
             p0(c)
-            if s == 4:
-                grad_piece(0, i)
-                grad_piece(1, i)
-            elif s == 5:
-                grad_piece(2, i)
-            elif s == 6:
-                grad_piece(3, i)
+            if s >= 4:
+                grad_piece(s - 4, i)
+                dp_slot((s - 4) * CHUNKS + i)
+            if s == 6:
+                for k in range(CHUNKS):
+                    @pl.when(i == k)
+                    def _(k=k):
+                        vec_step(k)
             return carry
         lax.fori_loop(0, CHUNKS, slot, 0)
         if s == 4:
@@ -494,10 +654,9 @@
             S["cv"][...] = S["dv"][...].astype(BF)
 
     last = STAGES - 1
-    g_copy = pltpu.make_async_copy(S["gbuf"], g_h, S["osem"].at[0])
-    g_copy.start()
     o_copy = pltpu.make_async_copy(S["outs"], out_h, S["osem"].at[1])
     o_copy.start()
+    vec_step(CHUNKS)
 
     p1(0)
     p2(last, 1)
@@ -511,8 +670,25 @@
     t_copy.start()
     m_copy = pltpu.make_async_copy(lows[6], mg_h, S["osem"].at[3])
     m_copy.start()
-    vg_h[...] = jnp.sum(S["vacc"][...], axis=1)
-    for x in (g_copy, o_copy, t_copy, m_copy):
+    for k in range(CHUNKS + 1, len(peers) + 1):
+        vec_step(k)
+    vg_h[...] = S["vsum"][...]
+
+    def tail_slot(j, carry):
+        @pl.when(j < pieces)
+        def _():
+            grad_piece(3, lax.rem(j, CHUNKS))
+        dp_slot(j)
+        return carry
+    lax.fori_loop(3 * CHUNKS, pieces + steps, tail_slot, 0)
+
+    def finish(p, carry, ff):
+        for x in result_copies(p, ff):
+            x.wait()
+        return carry
+    lax.fori_loop(0, 2 * CHUNKS, lambda p, x: finish(p, x, True), 0)
+    lax.fori_loop(2 * CHUNKS, pieces, lambda p, x: finish(p, x, False), 0)
+    for x in (o_copy, t_copy, m_copy):
         x.wait()
 
 
@@ -529,50 +705,45 @@
     lens = jnp.concatenate([decoder_length, memory_length])
     vec = jnp.stack([self_gain, self_bias, cross_gain, cross_bias, feed_gain, feed_bias,
                      feed_gain, feed_bias])
-    scratch = layout(rows, slots, width, inner, hidden)
+    copies = lax.axis_size("dp")
+    scratch = layout(rows, slots, width, inner, hidden, copies)
     names = tuple(scratch)
     given = dict(tok=tokens, mem=memory, wq=self_query, wk=self_key, wv=self_value,
                  wo=self_output, cwq=cross_query, cwk=cross_key, cwv=cross_value,
                  cwo=cross_output, win=feed_in, wout=feed_out)
     any_spec = pl.BlockSpec(memory_space=pl.ANY)
-    total = 2 * hidden + 2 * width
 
     def kernel(*refs):
-        layer_kernel(names, *refs)
-
-    out, tg, mg, g, vg = pl.pallas_call(
+        layer_kernel(names, copies, *refs)
+
+    out, tg, mg, gf, gq, go, vg = pl.pallas_call(
         kernel,
         out_shape=(
             jax.ShapeDtypeStruct((rows, width), BF),
             jax.ShapeDtypeStruct((rows, width), BF),
             jax.ShapeDtypeStruct((slots, width), BF),
-            jax.ShapeDtypeStruct((total, width), BF),
+            jax.ShapeDtypeStruct((2 * hidden, width), BF),
+            jax.ShapeDtypeStruct((2, 3, width, inner), BF),
+            jax.ShapeDtypeStruct((2, inner, width), BF),
             jax.ShapeDtypeStruct((8, width), F32),
         ),
         in_specs=[pl.BlockSpec(memory_space=pltpu.SMEM), pl.BlockSpec(memory_space=pltpu.VMEM)]
         + [any_spec] * (len(INPUTS) + 1),
-        out_specs=(any_spec,) * 4 + (pl.BlockSpec(memory_space=pltpu.VMEM),),
+        out_specs=(any_spec,) * 6 + (pl.BlockSpec(memory_space=pltpu.VMEM),),
         scratch_shapes=list(scratch.values()),
         compiler_params=pltpu.CompilerParams(
             collective_id=0, has_side_effects=True, vmem_limit_bytes=67043328),
         name="layer",
     )(lens, vec, *[given[n] for n in INPUTS], cotangent)
 
-    vecs = lax.psum(vg, ("dp", "tensor"))
-    grads = lax.psum(g, "dp").astype(F32)
-
-    def block(start):
-        x = grads[start:start + width]
-        return (x[:, :inner], x[:, inner:2 * inner], x[:, 2 * inner:3 * inner],
-                x[:, 3 * inner:].T)
-
-    cq, ck, cv, co = block(2 * hidden)
-    sq, sk, sv, so = block(2 * hidden + width)
+    def wide_grads(j):
+        return tuple(gq[j, i].astype(F32) for i in range(3)) + (go[j].astype(F32),)
+
     return (
         out, tg.astype(F32), mg.astype(F32),
-        sq, sk, sv, so, vecs[0], vecs[1],
-        cq, ck, cv, co, vecs[2], vecs[3],
-        grads[hidden:2 * hidden], grads[:hidden], vecs[4], vecs[5],
+        *wide_grads(1), vg[0], vg[1],
+        *wide_grads(0), vg[2], vg[3],
+        gf[hidden:].astype(F32), gf[:hidden].astype(F32), vg[4], vg[5],
     )
 
 

time: 553 us -> 369 us (0.67)
  waiting for transfers between devices: 220 us -> 0 us
  Pallas kernels: 235 us -> 346 us
  blocking collectives: 44.7 us -> 0 us
  local copies, waits for them, and re-layouts: 20.7 us -> 4.21 us
  between operations: 15.4 us -> 1.99 us
    psum x1 -> x0, waiting for transfers between devices: 220 us -> none  [shards(): grads = lax.psum(g, 'dp').astype(F32)]
    pallas_call x1, Pallas kernels: 235 us -> 346 us  [shards(): pl.pallas_call(kernel, out_shape=(jax.ShapeDtypeStruct((rows, width), BF)...]
    psum x1 -> x0, blocking collectives: 44.7 us -> none  [shards(): vecs = lax.psum(vg, ('dp', 'tensor'))]
    slice x3 -> x1, local copies, waits for them, and re-layouts: 12.1 us -> 0.62 us  [shards(): vg[5]]
    convert_element_type x1 -> x3, other arithmetic: 11.3 us -> 10.7 us  [the longest x1 4.73 us: wide_grads(): gq[j, i].astype(F32)]
  transfers between devices with their start and end apart: 1 -> 0, of which waited for: 1 -> 0; matrix products, arithmetic and copies ran while one was open for 1% -> 0% of each run, Pallas kernels for 0% -> 0%
where the time goes in v2:
time: 369 us
  Pallas kernels  346 us (94%)
  other arithmetic  16.3 us (4%)
  local copies, waits for them, and re-layouts  4.21 us (1%)
    pallas_call x1, Pallas kernels, shards(): pl.pallas_call(kernel, out_shape=(jax.ShapeDtypeStruct((rows, width), BF)...  346 us

profile of v2, /device:TPU:0, one launch (start us, length us, event | category | flops | bytes accessed | tf_op | source)
XLA Modules:
  0.0 368.6 jit_solution(7394745002598259162)
XLA Ops:
  0.7 1.5 stack.29.refs_1_
  3.4 0.6 pad_add_fusion.refs_0_
  4.0 346.2 %layer.1 = (bf16[1024,1024]{1,0:T(8,128)(2,1)}, bf16[1024,1024]{1,0:T(8,128)(2,1)}, bf16[1024,1024]{1,0:T(8,128)(2,1)}, bf16[2048,1024]{1,0:T(8,128)(2,1)}, bf16...) custom-call(s32[2]{0:T(128)} %pad_add_fusion.refs_0_, f32[8,1024]{1,0:T(8,128)} %stack.29.refs_1_, ...), custom_call_target="tpu_custom_call" | custom-call | tf_op jit(solution)/shard_map/layer/pallas_call | solution.py:719
  350.2 0.0 copy-start.5
  350.2 0.0 copy-start
  350.2 4.7 %bitcast_convert_fusion.1 = (f32[1024,256]{1,0:T(8,128)}, f32[1024,256]{1,0:T(8,128)}, f32[1024,256]{1,0:T(8,128)}, f32[1024,256]{1,0:T(8,128)}, f32[1024,256]{1,0:T(8,128)}, /*index=5*/f32[1024,256]{1,0:T(8,128)}) fusion(bf16[2,3,1024,256]{3,2,1,0:T(8,128)(2,1)} %get-tuple-element.29), kind=kLoop, calls=%fused_computation.3 | loop fusion | flops 1572864 | bytes 9437184 | tf_op jit(solution)/shard_map/convert_element_type | solution.py:740
  354.9 0.0 copy-done.5
  354.9 0.6 fusion
  355.5 0.0 copy-done
  355.5 0.0 copy-start.4
  355.5 4.4 %slice_convert_fusion = (f32[1024,1024]{1,0:T(8,128)}, f32[1024,1024]{1,0:T(8,128)}) fusion(bf16[2048,1024]{1,0:T(8,128)(2,1)S(1)} %copy-done), kind=kLoop, calls=%fused_computation | loop fusion | flops 2097152 | bytes 12582912 | tf_op jit(solution)/shard_map/convert_element_type | solution.py:746
  360.0 0.0 copy-start.2
  360.0 0.0 copy-done.4
  360.0 1.6 bitcast_convert_fusion
  361.5 0.8 copy-done.2
  362.3 0.0 copy-start.1
  362.3 2.5 convert_element_type.60
  364.8 0.0 copy-done.1
  364.8 0.0 copy-start.3
  364.8 2.5 convert_element_type.61
  367.3 0.0 copy-done.3
  367.3 1.3 copy.43
Async XLA Ops:
  350.2 4.8 %copy-start.5 = (f32[8,1024]{1,0:T(8,128)S(1)}, f32[8,1024]{1,0:T(8,128)}, u32[]{:S(2)}) copy-start(f32[8,1024]{1,0:T(8,128)} %get-tuple-element.31) | copy-start | bytes 98308
  350.2 5.4 %copy-start = (bf16[2048,1024]{1,0:T(8,128)(2,1)S(1)}, bf16[2048,1024]{1,0:T(8,128)(2,1)}, u32[]{:S(2)}) copy-start(bf16[2048,1024]{1,0:T(8,128)(2,1)} %get-tuple-element.32) | copy-start | bytes 12582916
  355.5 4.4 %copy-start.4 = (bf16[2,256,1024]{2,1,0:T(8,128)(2,1)S(1)}, bf16[2,256,1024]{2,1,0:T(8,128)(2,1)}, u32[]{:S(2)}) copy-start(bf16[2,256,1024]{2,1,0:T(8,128)(2,1)} %get-tuple-element.30) | copy-start | bytes 3145732
  360.0 2.3 copy-start.2
  362.3 2.5 copy-start.1
  364.8 2.5 copy-start.3

commit v3 on v2

--- a/solution.py
+++ b/solution.py
@@ -181,31 +181,24 @@
     S["cvt"][:, HD:, :] = jnp.ones((heads, 16, slots), BF)
     S["vacc"][...] = jnp.zeros(S["vacc"].shape, F32)
 
+    pl.semaphore_wait(barrier, 2 + bits)
+
     def wait_for(*which):
         for n in which:
             loads[n].wait()
 
-    def project(src, wk, wv, kd, vd, ktd, vtd, count):
-        def body(i, carry):
-            r = row(i)
-            x = src[r, :]
-            kf = mm(x, wk[...])
-            kd[r, :] = kf.astype(BF)
-            kt = kf.T.astype(BF)
-            vf = mm(x, wv[...])
-            vd[r, :] = vf.astype(BF)
-            vtt = vf.T.astype(BF)
-            for h in range(heads):
-                ktd[h, :, r] = kt[h * HD:(h + 1) * HD, :]
-                vtd[h, :HD, r] = vtt[h * HD:(h + 1) * HD, :]
-            return carry
-        lax.fori_loop(0, count, body, 0)
-
-    def project_q(src, w, dst):
-        def body(i, carry):
-            dst[row(i), :] = mm(src[row(i), :], w[...]).astype(BF)
-            return carry
-        lax.fori_loop(0, CHUNKS, body, 0)
+    def project(c, src, wk, wv, kd, vd, ktd, vtd):
+        r = row(c)
+        x = src[r, :]
+        kf = mm(x, wk[...])
+        kd[r, :] = kf.astype(BF)
+        kt = kf.T.astype(BF)
+        vf = mm(x, wv[...])
+        vd[r, :] = vf.astype(BF)
+        vtt = vf.T.astype(BF)
+        for h in range(heads):
+            ktd[h, :, r] = kt[h * HD:(h + 1) * HD, :]
+            vtd[h, :HD, r] = vtt[h * HD:(h + 1) * HD, :]
 
     def lanes(h):
         return pl.ds(pl.multiple_of((h // 2) * 2 * HD, 2 * HD), 2 * HD)
@@ -222,12 +215,12 @@
             ok = ok & (kid <= qid)
         return jnp.where(ok, scores * scale, NEGATIVE)
 
-    def head_forward(h, c, q, k, vt, lse, causal, length):
+    def head_forward(h, c, q, k, vt, lse, causal, length, keys):
         qm = pick(q[row(c), lanes(h)], h)
-        s = masked(mt(k[:, lanes(h)], qm), c, causal, length)
+        s = masked(mt(k[:keys, lanes(h)], qm), c, causal, length)
         top = jnp.max(s, axis=0, keepdims=True)
         p = jnp.exp(s - top).astype(BF)
-        o = mm(vt[h], p)
+        o = mm(vt[h, :, :keys], p)
         total = o[HD:HD + 1, :]
         S["flat"][pl.ds(pl.multiple_of(h * HD, HD), HD), :] = o[:HD, :] / total
         lse[c, h] = top + jnp.log(total)
@@ -281,12 +274,15 @@
     def compute(s, c, middle):
         part = S["part"]
         if s == 0:
-            each_head(lambda h: head_forward(h, c, S["q"], S["k"], S["vt"], S["lse"], True, dec), middle)
+            project(c, S["tok"], S["wk"], S["wv"], S["k"], S["v"], S["kt"], S["vt"])
+            S["q"][row(c), :] = mm(S["tok"][row(c), :], S["wq"][...]).astype(BF)
+            each_head(lambda h: head_forward(h, c, S["q"], S["k"], S["vt"], S["lse"], True, dec,
+                                             (c + 1) * R), middle)
             S["mixed"][row(c), :] = unflatten().astype(BF)
             wide(lambda n: mm(S["mixed"][row(c), :], S["wo"][:, n]), part, c)
         elif s == 1:
             S["cq"][row(c), :] = mm(S["low0"][row(c), :], S["cwq"][...]).astype(BF)
-            each_head(lambda h: head_forward(h, c, S["cq"], S["ck"], S["cvt"], S["clse"], False, enc), middle)
+            each_head(lambda h: head_forward(h, c, S["cq"], S["ck"], S["cvt"], S["clse"], False, enc, slots), middle)
             S["cmixed"][row(c), :] = unflatten().astype(BF)
             wide(lambda n: mm(S["cmixed"][row(c), :], S["cwo"][:, n]), part, c)
         elif s == 2:
@@ -389,7 +385,7 @@
     def p2(s, c):
         y_part(c).wait()
         if s == 2:
-            @pl.when(c == CHUNKS - 1)
+            @pl.when(c == 0)
             def _():
                 for x in cots:
                     x.wait()
@@ -434,21 +430,14 @@
         lax.fori_loop(0, Q // step, body, 0)
         gather(buf, c, 0, 2).start()
         gather(buf, c, 1, 2).start()
-        if s == 2:
-            gather(S["outs"], c, 0, 5).start()
-            gather(S["outs"], c, 1, 5).start()
 
     def p3(s, c):
-        sets = ((lows[s], 2), (S["outs"], 5)) if s == 2 else ((lows[s], 2),)
-        for buf, base in sets:
-            gather(buf, c, 0, base).wait()
-            gather(buf, c, 2, base).start()
+        gather(lows[s], c, 0, 2).wait()
+        gather(lows[s], c, 2, 2).start()
 
     def p4(s, c):
-        sets = ((lows[s], 2), (S["outs"], 5)) if s == 2 else ((lows[s], 2),)
-        for buf, base in sets:
-            gather(buf, c, 1, base).wait()
-            gather(buf, c, 2, base).wait()
+        gather(lows[s], c, 1, 2).wait()
+        gather(lows[s], c, 2, 2).wait()
 
     def grad_piece(g, i):
         n = pl.ds(pl.multiple_of(i * PIECE, PIECE), PIECE)
@@ -570,13 +559,19 @@
                 for x in result_copies(p, False):
                     x.start()
 
-    dp_order = [0] + [k for k in range(steps - 1, 1, -1)] + [steps, 1]
-
-    def dp_slot(j):
-        for k in dp_order:
-            p = j - k
-
-            @pl.when((p >= 0) & (p < pieces))
+    lag = [0, 2] + [2 + k for k in range(1, steps - 1)] + [steps + 2]
+    FIRST = 2 * CHUNKS
+    GAP = FIRST + 2
+    LAST = GAP + 4 * CHUNKS - 2
+
+    def dp_slot(m):
+        for k in [steps] + list(range(steps - 1, 1, -1)) + [0, 1]:
+            e = m - lag[k]
+            early = e < FIRST
+            p = jnp.where(early, e, FIRST + lax.div(e - GAP, 2))
+
+            @pl.when((e >= 0) & (e <= LAST)
+                     & (early | ((e >= GAP) & (lax.rem(e, 2) == 0))))
             def _(k=k, p=p):
                 dp_step(k, p)
 
@@ -596,91 +591,152 @@
         if k < len(peers):
             vec_copy(k).start()
 
-    wait_for("tok", "wk", "wv", "wq")
-    project(S["tok"], S["wk"], S["wv"], S["k"], S["v"], S["kt"], S["vt"], CHUNKS)
-    project_q(S["tok"], S["wq"], S["q"])
-    pl.semaphore_wait(barrier, 2 + bits)
-    wait_for("wo")
-
-    def lagged(i, lag, fn, s):
-        c = lax.rem(CHUNKS - 1 - i + lag, CHUNKS)
-
-        @pl.when(i >= lag)
+    def chunk_of(s, i):
+        return i if s <= 4 else CHUNKS - 1 - i
+
+    def lagged(i, n, fn, s):
+        def now():
+            fn(s, chunk_of(s, i - n))
+
+        def before():
+            fn(s - 1, chunk_of(s - 1, i - n + CHUNKS))
+        fresh = s in (0, 5)
+        if isinstance(i, int):
+            if i >= n:
+                now()
+            elif not fresh:
+                before()
+            return
+        pl.when(i >= n)(now)
+        if not fresh:
+            pl.when(i < n)(before)
+
+    def phases(i, s):
+        lagged(i, 3, p3, s)
+        lagged(i, 2, p2, s)
+        lagged(i, 1, lambda _, c: p1(c), s)
+
+    def ff_piece(m):
+        @pl.when(m < CHUNKS)
         def _():
-            fn(s, c)
+            grad_piece(0, m)
+
+        @pl.when(m >= CHUNKS)
+        def _():
+            grad_piece(1, m - CHUNKS)
+
+    def slot(i, s):
+        c = chunk_of(s, i)
         if s > 0:
-            @pl.when(i < lag)
-            def _():
-                fn(s - 1, c)
-
-    for s in range(STAGES):
+            p4(s - 1, c)
+        if s == 5:
+            gather(S["outs"], c, 0, 5).start()
+            gather(S["outs"], c, 1, 5).start()
+
+        def middle():
+            phases(i, s)
+            if s == 4:
+                ff_piece(2 * i)
+                dp_slot(2 * i)
+            elif s > 4:
+                grad_piece(s - 3, i)
+                dp_slot(GAP + 2 * CHUNKS * (s - 5) + 2 * i)
+            if s == 6:
+                gather(S["outs"], c, 0, 5).wait()
+                gather(S["outs"], c, 2, 5).start()
+                for k in range(CHUNKS):
+                    @pl.when(i == k)
+                    def _(k=k):
+                        vec_step(k)
+        compute(s, c, middle)
+        p0(c)
+        if s == 4:
+            ff_piece(2 * i + 1)
+            dp_slot(2 * i + 1)
+        elif s > 4:
+            dp_slot(GAP + 2 * CHUNKS * (s - 5) + 2 * i + 1)
+
+    def drain(s, t):
+        a, b, d = (chunk_of(s, i) for i in (1, 2, 3))
+
+        @pl.when(t == 0)
+        def _():
+            p3(s, a)
+            p2(s, b)
+            p1(d)
+
+        @pl.when(t == 1)
+        def _():
+            p3(s, b)
+            p2(s, d)
+
+        @pl.when(t == 2)
+        def _():
+            p3(s, d)
+
+    wait_for("tok", "wk", "wv", "wq", "wo")
+    for i in range(CHUNKS):
+        slot(i, 0)
+        if i == 0:
+            wait_for("mem", "cwk", "cwv")
+        project(i, S["mem"], S["cwk"], S["cwv"], S["ck"], S["cv"], S["ckt"], S["cvt"])
+
+    for s in range(1, STAGES):
         if s == 1:
-            wait_for("mem", "cwk", "cwv", "cwq", "cwo")
-            project(S["mem"], S["cwk"], S["cwv"], S["ck"], S["cv"], S["ckt"], S["cvt"], CHUNKS)
+            wait_for("cwq", "cwo")
         if s == 2:
             wait_for("win", "wout")
         if s in (4, 5):
             S["dk"][...] = jnp.zeros(S["dk"].shape, F32)
             S["dv"][...] = jnp.zeros(S["dv"].shape, F32)
 
-        def slot(i, carry, s=s):
-            c = CHUNKS - 1 - i
-            if s > 0:
-                p4(s - 1, c)
-
-            def middle():
-                lagged(i, 3, p3, s)
-                lagged(i, 2, p2, s)
-                if s > 0:
-                    p1(lax.rem(c + 1, CHUNKS))
-                else:
-                    @pl.when(i >= 1)
-                    def _():
-                        p1(lax.rem(c + 1, CHUNKS))
-            compute(s, c, middle)
-            p0(c)
-            if s >= 4:
-                grad_piece(s - 4, i)
-                dp_slot((s - 4) * CHUNKS + i)
-            if s == 6:
-                for k in range(CHUNKS):
-                    @pl.when(i == k)
-                    def _(k=k):
-                        vec_step(k)
+        def body(i, carry, s=s):
+            slot(i, s)
             return carry
-        lax.fori_loop(0, CHUNKS, slot, 0)
+        lax.fori_loop(0, CHUNKS, body, 0)
         if s == 4:
             S["ck"][...] = (S["dk"][...] * scale).astype(BF)
             S["cv"][...] = S["dv"][...].astype(BF)
 
+            def between(t, carry):
+                drain(4, t)
+
+                @pl.when(t < 2)
+                def _():
+                    dp_slot(FIRST + t)
+                return carry
+            lax.fori_loop(0, 3, between, 0)
+
     last = STAGES - 1
-    o_copy = pltpu.make_async_copy(S["outs"], out_h, S["osem"].at[1])
-    o_copy.start()
-    vec_step(CHUNKS)
-
-    p1(0)
-    p2(last, 1)
-    p3(last, 2)
-    p2(last, 0)
-    p3(last, 1)
-    p3(last, 0)
-    for c in range(CHUNKS):
-        p4(last, CHUNKS - 1 - c)
-    t_copy = pltpu.make_async_copy(lows[5], tg_h, S["osem"].at[2])
-    t_copy.start()
-    m_copy = pltpu.make_async_copy(lows[6], mg_h, S["osem"].at[3])
-    m_copy.start()
-    for k in range(CHUNKS + 1, len(peers) + 1):
-        vec_step(k)
+    tail = LAST + 2
+    outputs = [pltpu.make_async_copy(a, b, S["osem"].at[j])
+               for j, (a, b) in enumerate(((S["outs"], out_h), (lows[5], tg_h), (lows[6], mg_h)))]
+
+    def ending(m, carry):
+        t = m - tail
+        drain(last, t)
+
+        @pl.when(t == 0)
+        def _():
+            for c in range(CHUNKS):
+                gather(S["outs"], c, 1, 5).wait()
+                gather(S["outs"], c, 2, 5).wait()
+            outputs[0].start()
+            outputs[1].start()
+
+        @pl.when(t == 3)
+        def _():
+            for c in range(CHUNKS):
+                p4(last, c)
+            outputs[2].start()
+        for k in range(CHUNKS, len(peers) + 1):
+            @pl.when(t == k - CHUNKS)
+            def _(k=k):
+                vec_step(k)
+        dp_slot(m)
+        return carry
+    lax.fori_loop(tail, LAST + lag[-1] + 1, ending, 0)
     vg_h[...] = S["vsum"][...]
-
-    def tail_slot(j, carry):
-        @pl.when(j < pieces)
-        def _():
-            grad_piece(3, lax.rem(j, CHUNKS))
-        dp_slot(j)
-        return carry
-    lax.fori_loop(3 * CHUNKS, pieces + steps, tail_slot, 0)
 
     def finish(p, carry, ff):
         for x in result_copies(p, ff):
@@ -688,7 +744,7 @@
         return carry
     lax.fori_loop(0, 2 * CHUNKS, lambda p, x: finish(p, x, True), 0)
     lax.fori_loop(2 * CHUNKS, pieces, lambda p, x: finish(p, x, False), 0)
-    for x in (o_copy, t_copy, m_copy):
+    for x in outputs:
         x.wait()
 
 

time: 369 us -> 367 us (level)
  no operation moved by 1% of the time
where the time goes in v3:
time: 367 us
  Pallas kernels  344 us (94%)
  other arithmetic  16.3 us (4%)
  local copies, waits for them, and re-layouts  4.21 us (1%)
    pallas_call x1, Pallas kernels, shards(): pl.pallas_call(kernel, out_shape=(jax.ShapeDtypeStruct((rows, width), BF)...  344 us

profile of v3, /device:TPU:0, one launch (start us, length us, event | category | flops | bytes accessed | tf_op | source)
XLA Modules:
  0.0 366.5 jit_solution(12727274630700693413)
XLA Ops:
  0.7 1.5 stack.29.refs_1_
  3.4 0.6 pad_add_fusion.refs_0_
  4.0 344.0 %layer.1 = (bf16[1024,1024]{1,0:T(8,128)(2,1)}, bf16[1024,1024]{1,0:T(8,128)(2,1)}, bf16[1024,1024]{1,0:T(8,128)(2,1)}, bf16[2048,1024]{1,0:T(8,128)(2,1)}, bf16...) custom-call(s32[2]{0:T(128)} %pad_add_fusion.refs_0_, f32[8,1024]{1,0:T(8,128)} %stack.29.refs_1_, ...), custom_call_target="tpu_custom_call" | custom-call | tf_op jit(solution)/shard_map/layer/pallas_call | solution.py:775
  348.1 0.0 copy-start.5
  348.1 0.0 copy-start
  348.1 4.7 %bitcast_convert_fusion.1 = (f32[1024,256]{1,0:T(8,128)}, f32[1024,256]{1,0:T(8,128)}, f32[1024,256]{1,0:T(8,128)}, f32[1024,256]{1,0:T(8,128)}, f32[1024,256]{1,0:T(8,128)}, /*index=5*/f32[1024,256]{1,0:T(8,128)}) fusion(bf16[2,3,1024,256]{3,2,1,0:T(8,128)(2,1)} %get-tuple-element.29), kind=kLoop, calls=%fused_computation.3 | loop fusion | flops 1572864 | bytes 9437184 | tf_op jit(solution)/shard_map/convert_element_type | solution.py:796
  352.8 0.0 copy-done.5
  352.8 0.6 fusion
  353.4 0.0 copy-done
  353.4 0.0 copy-start.4
  353.4 4.4 %slice_convert_fusion = (f32[1024,1024]{1,0:T(8,128)}, f32[1024,1024]{1,0:T(8,128)}) fusion(bf16[2048,1024]{1,0:T(8,128)(2,1)S(1)} %copy-done), kind=kLoop, calls=%fused_computation | loop fusion | flops 2097152 | bytes 12582912 | tf_op jit(solution)/shard_map/convert_element_type | solution.py:802
  357.9 0.0 copy-start.2
  357.9 0.0 copy-done.4
  357.9 1.6 bitcast_convert_fusion
  359.4 0.8 copy-done.2
  360.2 0.0 copy-start.1
  360.2 2.5 convert_element_type.60
  362.7 0.0 copy-done.1
  362.7 0.0 copy-start.3
  362.7 2.5 convert_element_type.61
  365.2 0.0 copy-done.3
  365.2 1.3 copy.43
Async XLA Ops:
  348.1 4.8 %copy-start.5 = (f32[8,1024]{1,0:T(8,128)S(1)}, f32[8,1024]{1,0:T(8,128)}, u32[]{:S(2)}) copy-start(f32[8,1024]{1,0:T(8,128)} %get-tuple-element.31) | copy-start | bytes 98308
  348.1 5.4 %copy-start = (bf16[2048,1024]{1,0:T(8,128)(2,1)S(1)}, bf16[2048,1024]{1,0:T(8,128)(2,1)}, u32[]{:S(2)}) copy-start(bf16[2048,1024]{1,0:T(8,128)(2,1)} %get-tuple-element.32) | copy-start | bytes 12582916
  353.4 4.4 %copy-start.4 = (bf16[2,256,1024]{2,1,0:T(8,128)(2,1)S(1)}, bf16[2,256,1024]{2,1,0:T(8,128)(2,1)}, u32[]{:S(2)}) copy-start(bf16[2,256,1024]{2,1,0:T(8,128)(2,1)} %get-tuple-element.30) | copy-start | bytes 3145732
  357.9 2.3 copy-start.2
  360.2 2.5 copy-start.1
  362.7 2.5 copy-start.3

commit v4 on v3

--- a/solution.py
+++ b/solution.py
@@ -28,7 +28,7 @@
 
 
 PIECE = 256
-RING = 8
+RING = 12
 
 
 def split_sizes(copies):
@@ -123,7 +123,10 @@
 )
 
 
-def layer_kernel(names, copies, lens, vec, *refs):
+def layer_kernel(names, copies, *refs):
+    dec_ref, enc_ref = refs[:2]
+    vec = refs[2:8]
+    refs = refs[8:]
     n_in = len(INPUTS)
     srcs = dict(zip(INPUTS, refs[:n_in]))
     cot_h = refs[n_in]
@@ -168,10 +171,8 @@
              for j, n in enumerate(INPUTS)}
     cots = [pltpu.make_async_copy(cot_h.at[own_rows(c)], S["cot"].at[c], S["cotsem"].at[c])
             for c in range(CHUNKS)]
-    for n in INPUTS:
+    for n in INPUTS[:5]:
         loads[n].start()
-    for c in cots:
-        c.start()
 
     barrier = pltpu.get_barrier_semaphore()
     for peer in [core, ypar] + [dp_peer(1 << j) for j in range(bits)]:
@@ -180,8 +181,6 @@
     S["vt"][:, HD:, :] = jnp.ones((heads, 16, rows), BF)
     S["cvt"][:, HD:, :] = jnp.ones((heads, 16, slots), BF)
     S["vacc"][...] = jnp.zeros(S["vacc"].shape, F32)
-
-    pl.semaphore_wait(barrier, 2 + bits)
 
     def wait_for(*which):
         for n in which:
@@ -259,8 +258,8 @@
         for h in range(heads):
             S["delta"][h] = d[h:h + 1, :]
 
-    dec = lens[0]
-    enc = lens[1]
+    dec = dec_ref[0]
+    enc = enc_ref[0]
 
     def each_head(fn, middle):
         def body(h, carry):
@@ -371,7 +370,7 @@
         center = x - mean(x)
         inv = lax.rsqrt(mean(center * center) + EPSILON)
         xhat = center * inv
-        return xhat, inv, xhat * vec[2 * j:2 * j + 1, :] + vec[2 * j + 1:2 * j + 2, :]
+        return xhat, inv, xhat * vec[2 * j][...] + vec[2 * j + 1][...]
 
     def fold(x):
         return jnp.sum(x.reshape(x.shape[0] // 8, 8, width), axis=0)
@@ -379,7 +378,7 @@
     def norm_back(e, xhat, inv, j):
         S["vacc"][2 * j] += fold(e * xhat)
         S["vacc"][2 * j + 1] += fold(e)
-        eg = e * vec[2 * j:2 * j + 1, :]
+        eg = e * vec[2 * j][...]
         return (eg - mean(eg) - xhat * mean(eg * xhat)) * inv
 
     def p2(s, c):
@@ -559,13 +558,13 @@
                 for x in result_copies(p, False):
                     x.start()
 
-    lag = [0, 2] + [2 + k for k in range(1, steps - 1)] + [steps + 2]
+    lag = [2 * k for k in range(steps + 1)]
     FIRST = 2 * CHUNKS
     GAP = FIRST + 2
     LAST = GAP + 4 * CHUNKS - 2
 
     def dp_slot(m):
-        for k in [steps] + list(range(steps - 1, 1, -1)) + [0, 1]:
+        for k in list(range(steps - 1, -1, -1)) + [steps]:
             e = m - lag[k]
             early = e < FIRST
             p = jnp.where(early, e, FIRST + lax.div(e - GAP, 2))
@@ -612,9 +611,9 @@
             pl.when(i < n)(before)
 
     def phases(i, s):
+        lagged(i, 1, lambda _, c: p1(c), s)
+        lagged(i, 2, p2, s)
         lagged(i, 3, p3, s)
-        lagged(i, 2, p2, s)
-        lagged(i, 1, lambda _, c: p1(c), s)
 
     def ff_piece(m):
         @pl.when(m < CHUNKS)
@@ -649,6 +648,8 @@
                     def _(k=k):
                         vec_step(k)
         compute(s, c, middle)
+        if s == 0 and i == 0:
+            pl.semaphore_wait(barrier, 2 + bits)
         p0(c)
         if s == 4:
             ff_piece(2 * i + 1)
@@ -675,6 +676,10 @@
             p3(s, d)
 
     wait_for("tok", "wk", "wv", "wq", "wo")
+    for n in INPUTS[5:]:
+        loads[n].start()
+    for x in cots:
+        x.start()
     for i in range(CHUNKS):
         slot(i, 0)
         if i == 0:
@@ -714,6 +719,7 @@
 
     def ending(m, carry):
         t = m - tail
+        dp_slot(m)
         drain(last, t)
 
         @pl.when(t == 0)
@@ -733,7 +739,6 @@
             @pl.when(t == k - CHUNKS)
             def _(k=k):
                 vec_step(k)
-        dp_slot(m)
         return carry
     lax.fori_loop(tail, LAST + lag[-1] + 1, ending, 0)
     vg_h[...] = S["vsum"][...]
@@ -746,6 +751,44 @@
     lax.fori_loop(2 * CHUNKS, pieces, lambda p, x: finish(p, x, False), 0)
     for x in outputs:
         x.wait()
+
+
+def widen(out, tg, mg, gf, gq, go):
+    parts = 8
+    width = out.shape[1]
+    hidden = gf.shape[0] // 2
+    inner = gq.shape[-1]
+    row_specs, shapes, ins, in_specs = [], [], [], []
+
+    def add(x, rows, columns, spec, dtype=F32):
+        ins.append(x)
+        in_specs.append(spec)
+        row_specs.append(pl.BlockSpec((rows // parts, columns), lambda i: (i, 0)))
+        shapes.append(jax.ShapeDtypeStruct((rows, columns), dtype))
+
+    for x, dtype in ((out, BF), (tg, F32), (mg, F32)):
+        n = x.shape[0]
+        add(x, n, width, pl.BlockSpec((n // parts, width), lambda i: (i, 0)), dtype)
+    for g in (1, 0):
+        for j in range(3):
+            add(gq, width, inner, pl.BlockSpec(
+                (None, None, width // parts, inner), lambda i, g=g, j=j: (g, j, i, 0)))
+        add(go, inner, width, pl.BlockSpec(
+            (None, inner // parts, width), lambda i, g=g: (g, i, 0)))
+    for g in range(2):
+        add(gf, hidden, width, pl.BlockSpec(
+            (hidden // parts, width), lambda i, g=g: (g * parts + i, 0)))
+
+    def body(*refs):
+        n = len(ins)
+        for a, b in zip(refs[:n], refs[n:]):
+            b[...] = a[...].astype(b.dtype)
+
+    return pl.pallas_call(
+        body, out_shape=tuple(shapes), grid=(parts,), in_specs=in_specs,
+        out_specs=tuple(row_specs), name="widen",
+        compiler_params=pltpu.CompilerParams(dimension_semantics=("arbitrary",)),
+    )(*ins)
 
 
 def shards(
@@ -758,9 +801,8 @@
     slots = memory.shape[0]
     inner = self_query.shape[1]
     hidden = feed_in.shape[1]
-    lens = jnp.concatenate([decoder_length, memory_length])
-    vec = jnp.stack([self_gain, self_bias, cross_gain, cross_bias, feed_gain, feed_bias,
-                     feed_gain, feed_bias])
+    vecs = [x.reshape(1, width) for x in (
+        self_gain, self_bias, cross_gain, cross_bias, feed_gain, feed_bias)]
     copies = lax.axis_size("dp")
     scratch = layout(rows, slots, width, inner, hidden, copies)
     names = tuple(scratch)
@@ -783,23 +825,21 @@
             jax.ShapeDtypeStruct((2, inner, width), BF),
             jax.ShapeDtypeStruct((8, width), F32),
         ),
-        in_specs=[pl.BlockSpec(memory_space=pltpu.SMEM), pl.BlockSpec(memory_space=pltpu.VMEM)]
-        + [any_spec] * (len(INPUTS) + 1),
+        in_specs=[pl.BlockSpec(memory_space=pltpu.SMEM)] * 2
+        + [pl.BlockSpec(memory_space=pltpu.VMEM)] * 6 + [any_spec] * (len(INPUTS) + 1),
         out_specs=(any_spec,) * 6 + (pl.BlockSpec(memory_space=pltpu.VMEM),),
         scratch_shapes=list(scratch.values()),
         compiler_params=pltpu.CompilerParams(
             collective_id=0, has_side_effects=True, vmem_limit_bytes=67043328),
         name="layer",
-    )(lens, vec, *[given[n] for n in INPUTS], cotangent)
-
-    def wide_grads(j):
-        return tuple(gq[j, i].astype(F32) for i in range(3)) + (go[j].astype(F32),)
-
+    )(decoder_length, memory_length, *vecs, *[given[n] for n in INPUTS], cotangent)
+
+    wide = widen(out, tg, mg, gf, gq, go)
     return (
-        out, tg.astype(F32), mg.astype(F32),
-        *wide_grads(1), vg[0], vg[1],
-        *wide_grads(0), vg[2], vg[3],
-        gf[hidden:].astype(F32), gf[:hidden].astype(F32), vg[4], vg[5],
+        *wide[:3],
+        *wide[3:7], vg[0], vg[1],
+        *wide[7:11], vg[2], vg[3],
+        wide[12], wide[11], vg[4], vg[5],
     )
 
 

time: 367 us -> 319 us (0.87)
  Pallas kernels: 344 us -> 314 us
  other arithmetic: 16.3 us -> 0 us
    pallas_call x1, Pallas kernels: 344 us -> 299 us  [shards(): pl.pallas_call(kernel, out_shape=(jax.ShapeDtypeStruct((rows, width), BF)...]
    convert_element_type x5 -> x0, other arithmetic: 15.7 us -> none  [the longest x1 4.73 us: wide_grads(): gq[j, i].astype(F32)]
    pallas_call x0 -> x1, Pallas kernels: none -> 15.2 us  [widen(): pl.pallas_call(body, out_shape=tuple(shapes), grid=(parts,), in_specs=in_...]
where the time goes in v4:
time: 319 us; the launch traced here: 318 us
  Pallas kernels  314 us (98%)
    pallas_call x1, Pallas kernels, shards(): pl.pallas_call(kernel, out_shape=(jax.ShapeDtypeStruct((rows, width), BF)...  299 us
    pallas_call x1, Pallas kernels, widen(): pl.pallas_call(body, out_shape=tuple(shapes), grid=(parts,), in_specs=in_...  15.2 us

profile of v4, /device:TPU:0, one launch (start us, length us, event | category | flops | bytes accessed | tf_op | source)
XLA Modules:
  0.0 318.0 jit_solution(13073568388235509907)
XLA Ops:
  2.0 299.2 %layer.1 = (bf16[1024,1024]{1,0:T(8,128)(2,1)}, bf16[1024,1024]{1,0:T(8,128)(2,1)}, bf16[1024,1024]{1,0:T(8,128)(2,1)}, bf16[2048,1024]{1,0:T(8,128)(2,1)}, bf16...) custom-call(s32[1]{0:T(128)S(6)} %copy.40.refs_0_, s32[1]{0:T(128)S(6)} %copy.41.refs_1_, ...), custom_call_target="tpu_custom_call" | custom-call | tf_op jit(solution)/shard_map/layer/pallas_call | solution.py:817
  301.1 1.6 fusion
  302.7 15.2 %widen.1 = (bf16[1024,1024]{1,0:T(8,128)(2,1)}, f32[1024,1024]{1,0:T(8,128)}, f32[1024,1024]{1,0:T(8,128)}, f32[1024,256]{1,0:T(8,128)}, f32[1024,256]{1,0:T(8,1...) custom-call(bf16[1024,1024]{1,0:T(8,128)(2,1)} %get-tuple-element.39, ...), custom_call_target="tpu_custom_call" | custom-call | tf_op jit(solution)/shard_map/widen/pallas_call | solution.py:787

commit v5 on v4

--- a/solution.py
+++ b/solution.py
@@ -29,6 +29,8 @@
 
 PIECE = 256
 RING = 12
+SWAPPED = 0b0101000000001010
+WAITS = (2, 2, 2, 3, 4, 4)
 
 
 def split_sizes(copies):
@@ -460,7 +462,7 @@
     def weight(step, p):
         if bits < 2 or step > 1:
             return 1 << step
-        swap = lax.div(lax.rem(p, 4), 3)
+        swap = lax.rem(lax.shift_right_logical(SWAPPED, p), 2)
         return 1 + swap if step == 0 else 2 - swap
 
     def start_of(step, p):
@@ -558,13 +560,14 @@
                 for x in result_copies(p, False):
                     x.start()
 
-    lag = [2 * k for k in range(steps + 1)]
+    waits = WAITS if steps == len(WAITS) else (2,) * steps
+    lag = [sum(waits[:k]) for k in range(steps + 1)]
     FIRST = 2 * CHUNKS
     GAP = FIRST + 2
     LAST = GAP + 4 * CHUNKS - 2
 
     def dp_slot(m):
-        for k in list(range(steps - 1, -1, -1)) + [steps]:
+        for k in range(steps + 1):
             e = m - lag[k]
             early = e < FIRST
             p = jnp.where(early, e, FIRST + lax.div(e - GAP, 2))
@@ -754,7 +757,7 @@
 
 
 def widen(out, tg, mg, gf, gq, go):
-    parts = 8
+    parts = 16
     width = out.shape[1]
     hidden = gf.shape[0] // 2
     inner = gq.shape[-1]

time: 319 us -> 295 us (0.925)
  Pallas kernels: 314 us -> 291 us
    pallas_call x1, Pallas kernels: 299 us -> 273 us  [shards(): pl.pallas_call(kernel, out_shape=(jax.ShapeDtypeStruct((rows, width), BF)...]
where the time goes in v5:
time: 295 us; the launch traced here: 294 us
  Pallas kernels  291 us (99%)
    pallas_call x1, Pallas kernels, shards(): pl.pallas_call(kernel, out_shape=(jax.ShapeDtypeStruct((rows, width), BF)...  273 us
    pallas_call x1, Pallas kernels, widen(): pl.pallas_call(body, out_shape=tuple(shapes), grid=(parts,), in_specs=in_...  18.1 us

profile of v5, /device:TPU:0, one launch (start us, length us, event | category | flops | bytes accessed | tf_op | source)
XLA Modules:
  0.0 294.4 jit_solution(15616613339413909524)
XLA Ops:
  2.0 272.5 %layer.1 = (bf16[1024,1024]{1,0:T(8,128)(2,1)}, bf16[1024,1024]{1,0:T(8,128)(2,1)}, bf16[1024,1024]{1,0:T(8,128)(2,1)}, bf16[2048,1024]{1,0:T(8,128)(2,1)}, bf16...) custom-call(s32[1]{0:T(128)S(6)} %copy.40.refs_0_, s32[1]{0:T(128)S(6)} %copy.41.refs_1_, ...), custom_call_target="tpu_custom_call" | custom-call | tf_op jit(solution)/shard_map/layer/pallas_call | solution.py:820
  274.5 1.6 fusion
  276.1 18.1 %widen.1 = (bf16[1024,1024]{1,0:T(8,128)(2,1)}, f32[1024,1024]{1,0:T(8,128)}, f32[1024,1024]{1,0:T(8,128)}, f32[1024,256]{1,0:T(8,128)}, f32[1024,256]{1,0:T(8,1...) custom-call(bf16[1024,1024]{1,0:T(8,128)(2,1)} %get-tuple-element.39, ...), custom_call_target="tpu_custom_call" | custom-call | tf_op jit(solution)/shard_map/widen/pallas_call | solution.py:790

commit v6 on v5

--- a/solution.py
+++ b/solution.py
@@ -29,8 +29,9 @@
 
 PIECE = 256
 RING = 12
-SWAPPED = 0b0101000000001010
-WAITS = (2, 2, 2, 3, 4, 4)
+SWAPPED = 0b1010000000010010
+WAITS = (3, 3, 2, 2, 3, 5)
+ORDER = (0, 1, 2, 3, 4, 5, 6)
 
 
 def split_sizes(copies):
@@ -563,11 +564,11 @@
     waits = WAITS if steps == len(WAITS) else (2,) * steps
     lag = [sum(waits[:k]) for k in range(steps + 1)]
     FIRST = 2 * CHUNKS
-    GAP = FIRST + 2
+    GAP = FIRST + 4
     LAST = GAP + 4 * CHUNKS - 2
 
     def dp_slot(m):
-        for k in range(steps + 1):
+        for k in ORDER if steps == len(WAITS) else range(steps + 1):
             e = m - lag[k]
             early = e < FIRST
             p = jnp.where(early, e, FIRST + lax.div(e - GAP, 2))
@@ -623,9 +624,13 @@
         def _():
             grad_piece(0, m)
 
-        @pl.when(m >= CHUNKS)
+        @pl.when((m >= CHUNKS) & (m < FIRST))
         def _():
             grad_piece(1, m - CHUNKS)
+
+    def ff_slot(m):
+        ff_piece(m)
+        dp_slot(m)
 
     def slot(i, s):
         c = chunk_of(s, i)
@@ -638,8 +643,7 @@
         def middle():
             phases(i, s)
             if s == 4:
-                ff_piece(2 * i)
-                dp_slot(2 * i)
+                ff_slot(2 * i + 2)
             elif s > 4:
                 grad_piece(s - 3, i)
                 dp_slot(GAP + 2 * CHUNKS * (s - 5) + 2 * i)
@@ -655,8 +659,7 @@
             pl.semaphore_wait(barrier, 2 + bits)
         p0(c)
         if s == 4:
-            ff_piece(2 * i + 1)
-            dp_slot(2 * i + 1)
+            ff_slot(2 * i + 3)
         elif s > 4:
             dp_slot(GAP + 2 * CHUNKS * (s - 5) + 2 * i + 1)
 
@@ -694,6 +697,12 @@
             wait_for("cwq", "cwo")
         if s == 2:
             wait_for("win", "wout")
+        if s == 4:
+            def ahead(m, carry):
+                grad_piece(0, m)
+                dp_slot(m)
+                return carry
+            lax.fori_loop(0, 2, ahead, 0)
         if s in (4, 5):
             S["dk"][...] = jnp.zeros(S["dk"].shape, F32)
             S["dv"][...] = jnp.zeros(S["dv"].shape, F32)
@@ -711,7 +720,7 @@
 
                 @pl.when(t < 2)
                 def _():
-                    dp_slot(FIRST + t)
+                    dp_slot(FIRST + 2 + t)
                 return carry
             lax.fori_loop(0, 3, between, 0)
 
@@ -756,42 +765,56 @@
         x.wait()
 
 
-def widen(out, tg, mg, gf, gq, go):
-    parts = 16
+def widen(out, tg, mg, gf, gq, go, vg):
+    parts = 8
     width = out.shape[1]
     hidden = gf.shape[0] // 2
     inner = gq.shape[-1]
-    row_specs, shapes, ins, in_specs = [], [], [], []
-
-    def add(x, rows, columns, spec, dtype=F32):
-        ins.append(x)
-        in_specs.append(spec)
-        row_specs.append(pl.BlockSpec((rows // parts, columns), lambda i: (i, 0)))
-        shapes.append(jax.ShapeDtypeStruct((rows, columns), dtype))
-
-    for x, dtype in ((out, BF), (tg, F32), (mg, F32)):
-        n = x.shape[0]
-        add(x, n, width, pl.BlockSpec((n // parts, width), lambda i: (i, 0)), dtype)
-    for g in (1, 0):
-        for j in range(3):
-            add(gq, width, inner, pl.BlockSpec(
-                (None, None, width // parts, inner), lambda i, g=g, j=j: (g, j, i, 0)))
-        add(go, inner, width, pl.BlockSpec(
-            (None, inner // parts, width), lambda i, g=g: (g, i, 0)))
-    for g in range(2):
-        add(gf, hidden, width, pl.BlockSpec(
-            (hidden // parts, width), lambda i, g=g: (g * parts + i, 0)))
-
-    def body(*refs):
-        n = len(ins)
-        for a, b in zip(refs[:n], refs[n:]):
-            b[...] = a[...].astype(b.dtype)
+    rows, slots = out.shape[0], mg.shape[0]
+
+    def tall(n, columns):
+        return pl.BlockSpec((n // parts, columns), lambda i: (i, 0))
+
+    shapes = [jax.ShapeDtypeStruct((rows, width), BF)]
+    shapes += [jax.ShapeDtypeStruct(x.shape, F32) for x in (tg, mg)]
+    out_specs = [tall(rows, width), tall(rows, width), tall(slots, width)]
+    for _ in range(2):
+        shapes += [jax.ShapeDtypeStruct((width, inner), F32)] * 3
+        shapes += [jax.ShapeDtypeStruct((inner, width), F32)]
+        out_specs += [tall(width, inner)] * 3 + [tall(inner, width)]
+    shapes += [jax.ShapeDtypeStruct((hidden, width), F32)] * 2
+    out_specs += [tall(hidden, width)] * 2
+    shapes += [jax.ShapeDtypeStruct((width,), F32)] * 6
+    out_specs += [pl.BlockSpec((width,), lambda i: (0,))] * 6
+
+    def body(o, t, m, q, w, f, v, *res):
+        res[0][...] = o[...]
+        res[1][...] = t[...].astype(F32)
+        res[2][...] = m[...].astype(F32)
+        for a, g in enumerate((1, 0)):
+            for j in range(3):
+                res[3 + 4 * a + j][...] = q[g, j].astype(F32)
+            res[6 + 4 * a][...] = w[g].astype(F32)
+        for g in range(2):
+            res[11 + g][...] = f[g].astype(F32)
+
+        @pl.when(pl.program_id(0) == 0)
+        def _():
+            for j in range(6):
+                res[13 + j][...] = v[j]
 
     return pl.pallas_call(
-        body, out_shape=tuple(shapes), grid=(parts,), in_specs=in_specs,
-        out_specs=tuple(row_specs), name="widen",
+        body, out_shape=tuple(shapes), grid=(parts,),
+        in_specs=[
+            tall(rows, width), tall(rows, width), tall(slots, width),
+            pl.BlockSpec((2, 3, width // parts, inner), lambda i: (0, 0, i, 0)),
+            pl.BlockSpec((2, inner // parts, width), lambda i: (0, i, 0)),
+            pl.BlockSpec((2, hidden // parts, width), lambda i: (0, i, 0)),
+            pl.BlockSpec((8, width), lambda i: (0, 0)),
+        ],
+        out_specs=tuple(out_specs), name="widen",
         compiler_params=pltpu.CompilerParams(dimension_semantics=("arbitrary",)),
-    )(*ins)
+    )(out, tg, mg, gq, go, gf.reshape(2, hidden, width), vg)
 
 
 def shards(
@@ -837,12 +860,12 @@
         name="layer",
     )(decoder_length, memory_length, *vecs, *[given[n] for n in INPUTS], cotangent)
 
-    wide = widen(out, tg, mg, gf, gq, go)
+    wide = widen(out, tg, mg, gf, gq, go, vg)
     return (
         *wide[:3],
-        *wide[3:7], vg[0], vg[1],
-        *wide[7:11], vg[2], vg[3],
-        wide[12], wide[11], vg[4], vg[5],
+        *wide[3:7], wide[13], wide[14],
+        *wide[7:11], wide[15], wide[16],
+        wide[12], wide[11], wide[17], wide[18],
     )
 
 

time: 295 us -> 287 us (0.973)
  Pallas kernels: 291 us -> 284 us
    pallas_call x1, Pallas kernels: 273 us -> 269 us  [shards(): pl.pallas_call(kernel, out_shape=(jax.ShapeDtypeStruct((rows, width), BF)...]
where the time goes in v6:
time: 287 us
  Pallas kernels  284 us (99%)
    pallas_call x1, Pallas kernels, shards(): pl.pallas_call(kernel, out_shape=(jax.ShapeDtypeStruct((rows, width), BF)...  269 us
    pallas_call x1, Pallas kernels, widen(): pl.pallas_call(body, out_shape=tuple(shapes), grid=(parts,), in_specs=[ta...  15.6 us

profile of v6, /device:TPU:0, one launch (start us, length us, event | category | flops | bytes accessed | tf_op | source)
XLA Modules:
  0.0 286.5 jit_solution(11577385190583750101)
XLA Ops:
  2.0 268.8 %layer.1 = (bf16[1024,1024]{1,0:T(8,128)(2,1)}, bf16[1024,1024]{1,0:T(8,128)(2,1)}, bf16[1024,1024]{1,0:T(8,128)(2,1)}, bf16[2048,1024]{1,0:T(8,128)(2,1)}, bf16...) custom-call(s32[1]{0:T(128)S(6)} %copy.40.refs_0_, s32[1]{0:T(128)S(6)} %copy.41.refs_1_, ...), custom_call_target="tpu_custom_call" | custom-call | tf_op jit(solution)/shard_map/layer/pallas_call | solution.py:843
  270.7 15.6 %widen.1 = (bf16[1024,1024]{1,0:T(8,128)(2,1)}, f32[1024,1024]{1,0:T(8,128)}, f32[1024,1024]{1,0:T(8,128)}, f32[1024,256]{1,0:T(8,128)}, f32[1024,256]{1,0:T(8,1...) custom-call(bf16[1024,1024]{1,0:T(8,128)(2,1)} %get-tuple-element.45, ...), custom_call_target="tpu_custom_call" | custom-call | tf_op jit(solution)/shard_map/widen/pallas_call | solution.py:806
